TPU v7x, 8 devices: a whole 2x2x1 slice. The times are simulated.
8 devices in a mesh: rep: 1 (over z), dp: 8 (over x, y, core).
Axes of the slice: x: 2, y: 2, z: 1, core: 2. Of those that a mesh axis runs over, the one named last changes fastest.
Arguments:
- x: bfloat16 [8, 2048, 1024], P(('rep', 'dp'))
- dy: bfloat16 [8, 2048, 1024], P(('rep', 'dp'))
- w_gate: bfloat16 [2, 1024, 2816], replicated
- w_up: bfloat16 [2, 1024, 2816], replicated
- w_down: bfloat16 [2, 2816, 1024], replicated
- m_w_gate: float32 [2, 1024, 2816], P(None, 'dp')
- m_w_up: float32 [2, 1024, 2816], P(None, 'dp')
- m_w_down: float32 [2, 2816, 1024], P(None, 'dp')
- v_w_gate: float32 [2, 1024, 2816], P(None, 'dp')
- v_w_up: float32 [2, 1024, 2816], P(None, 'dp')
- v_w_down: float32 [2, 2816, 1024], P(None, 'dp')
Outputs:
- output 1: bfloat16 [2, 1024, 2816], P('rep')
- output 2: bfloat16 [2, 1024, 2816], P('rep')
- output 3: bfloat16 [2, 2816, 1024], P('rep')
- output 4: float32 [2, 1024, 2816], P('rep', 'dp')
- output 5: float32 [2, 1024, 2816], P('rep', 'dp')
- output 6: float32 [2, 2816, 1024], P('rep', 'dp')
- output 7: float32 [2, 1024, 2816], P('rep', 'dp')
- output 8: float32 [2, 1024, 2816], P('rep', 'dp')
- output 9: float32 [2, 2816, 1024], P('rep', 'dp')
All inputs are finite; a program needn't handle non-finite values.
Results may differ from a plain program's by a relative error of at most 0.022.
Values are sent between devices in bfloat16 or wider.
A program may use at most 2 GiB of HBM per device.

v0:
```python
import jax
import jax.numpy as jnp
from jax import lax
from jax.experimental import pallas as pl
from jax.experimental.pallas import tpu as pltpu


BF, F32 = jnp.bfloat16, jnp.float32
NB = 256
VM = 64 * 1024 * 1024 - 65536


def dot(a, b, ca=1, cb=0):
    return lax.dot_general(a, b, (((ca,), (cb,)), ((), ())), preferred_element_type=F32)


def normed(h):
    wide = h.astype(F32)
    scale = lax.rsqrt(jnp.mean(wide * wide, -1, keepdims=True) + 1e-6)
    return (wide * scale).astype(BF)


def params():
    return pltpu.CompilerParams(vmem_limit_bytes=VM, dimension_semantics=("arbitrary",))


def whole(shape):
    return pl.BlockSpec(shape, lambda j: (0,) * len(shape))


def cost(mm, by):
    return pl.CostEstimate(flops=mm, bytes_accessed=by, transcendentals=0)


def tiles(t, rt):
    return [pl.ds(i * rt, rt) for i in range(t // rt)]


def beside(ref, one, other):
    n = one.shape[1]
    ref[:, :n] = one[...]
    ref[:, n:] = other[...]


def fwd0(x, wg, wu, wd, layer):
    t_, d = x.shape
    ff = wg.shape[2]
    n1, rt = ff // NB, 512
    n2 = t_ // rt

    def body(x_hbm, wg_ref, wu_ref, wd_hbm, gate_ref, up_ref, a_hbm, h_ref, b_ref, xs, a, hid, w, wds, sem, wd_sem, a_sem):
        t = pl.program_id(0)
        wd_load = pltpu.make_async_copy(wd_hbm.at[layer], wds, wd_sem)
        a_store = pltpu.make_async_copy(a, a_hbm, a_sem)

        @pl.when(t == 0)
        def _():
            loads = [pltpu.make_async_copy(x_hbm.at[r], xs.at[r], sem.at[i]) for i, r in enumerate(tiles(t_, rt))]
            for load in loads:
                load.start()
            wd_load.start()
            for i, load in enumerate(loads):
                load.wait()
                for r in range(i * rt, (i + 1) * rt, 256):
                    a[pl.ds(r, 256), :] = normed(xs[pl.ds(r, 256), :])

        @pl.when(t == 1)
        def _():
            a_store.start()

        @pl.when(t < n1)
        def _():
            beside(w, wg_ref, wu_ref)
            cols = pl.ds(pl.multiple_of(t * NB, NB), NB)
            for r in tiles(t_, rt):
                both = dot(a[r, :], w[...])
                gate, up = both[:, :NB], both[:, NB:]
                gate_ref[r, :] = gate
                up_ref[r, :] = up
                hid[r, cols] = (jax.nn.silu(gate) * up).astype(BF)

        @pl.when(t == n1)
        def _():
            wd_load.wait()
            a_store.wait()

        @pl.when(t >= n1)
        def _():
            r = pl.ds(pl.multiple_of((t - n1) * rt, rt), rt)
            h = xs[r, :] + dot(hid[r, :], wds[...]).astype(BF)
            h_ref[...] = h
            b_ref[...] = normed(h)

    def block(j):
        return jnp.minimum(j, n1 - 1)

    anyw = pl.BlockSpec(memory_space=pl.ANY)
    wcol = pl.BlockSpec((None, d, NB), lambda j: (layer, 0, block(j)))
    gcol = pl.BlockSpec((t_, NB), lambda j: (0, block(j)))
    hrow = pl.BlockSpec((rt, d), lambda j: (jnp.maximum(j - n1, 0), 0))
    return pl.pallas_call(
        body,
        grid=(n1 + n2,),
        in_specs=[anyw, wcol, wcol, anyw],
        out_specs=[gcol, gcol, anyw, hrow, hrow],
        out_shape=[jax.ShapeDtypeStruct((t_, ff), F32)] * 2 + [jax.ShapeDtypeStruct((t_, d), BF)] * 3,
        scratch_shapes=[
            pltpu.VMEM((t_, d), BF),
            pltpu.VMEM((t_, d), BF),
            pltpu.VMEM((t_, ff), BF),
            pltpu.VMEM((d, 2 * NB), BF),
            pltpu.VMEM((ff, d), BF),
            pltpu.SemaphoreType.DMA((n2,)),
            pltpu.SemaphoreType.DMA,
            pltpu.SemaphoreType.DMA,
        ],
        compiler_params=params(),
        cost_estimate=cost(6 * t_ * d * ff, 0),
        name="forward0",
    )(x, wg, wu, wd)


def hidden_back(dh, gate, up):
    s = jax.nn.sigmoid(gate)
    sg = gate * s
    return (dh * up * (s + sg * (1 - s))).astype(BF), (dh * sg).astype(BF), sg


SRC, RC, SX, RX, S2, R2 = 4, 5, 2, 6, 2, 4
MESH = pl.DeviceIdType.MESH
GU, DD = 256, 352


class Exchange:
    def __init__(self, src, rc, sx, sy, rx, ry, s2, r2, sent, got, squares, put):
        self.src, self.rc, self.sx, self.sy, self.rx, self.ry, self.s2, self.r2 = src, rc, sx, sy, rx, ry, s2, r2
        self.sent, self.got, self.squares, self.put = sent, got, squares, put
        me = lax.axis_index("dp")
        self.x, self.y, self.c = me // 4, me // 2 % 2, me % 2
        self.over_c, self.over_y, self.over_x = me + 1 - 2 * self.c, me + 2 - 4 * self.y, me + 4 - 8 * self.x

    def barrier(self):
        b = pltpu.get_barrier_semaphore()
        for other in (self.over_c, self.over_y, self.over_x):
            pl.semaphore_signal(b, inc=1, device_id={"dp": other}, device_id_type=MESH)
        pl.semaphore_wait(b, 3)

    def copy(self, n, slot, src, dst, other):
        return pltpu.make_async_remote_copy(
            src_ref=src, dst_ref=dst, send_sem=self.sent.at[n, slot], recv_sem=self.got.at[n, slot],
            device_id={"dp": other}, device_id_type=MESH,
        )

    def copies(self, stage, k, rows):
        h = rows // 2
        if stage == 0:
            s, r = lax.rem(k, SRC), lax.rem(k, RC)
            return [self.copy(0, r, self.src.at[s, :, 1 - self.c, :rows], self.rc.at[r, :, :rows], self.over_c)]
        if stage == 1:
            s, r = lax.rem(k, SX), lax.rem(k, RX)
            return [
                self.copy(1, r, self.sx.at[s, :, :h], self.rx.at[r, :, :h], self.over_x),
                self.copy(2, r, self.sy.at[s, :, :h], self.ry.at[r, :, :h], self.over_y),
            ]
        s, r = lax.rem(k, S2), lax.rem(k, R2)
        return [
            self.copy(3, r, self.s2.at[s, 0, :h], self.r2.at[r, 0, :h], self.over_y),
            self.copy(4, r, self.s2.at[s, 1, :h], self.r2.at[r, 1, :h], self.over_x),
        ]

    def start(self, stage, k, rows):
        for c in self.copies(stage, k, rows):
            c.start()

    def chip(self, k, i, j, part):
        at = i * 2 + j
        return self.src[lax.rem(k, SRC), at, self.c, part, :].astype(F32) + self.rc[lax.rem(k, RC), at, part, :].astype(F32)

    def stage(self, n, k, rows):
        for c in self.copies(n - 1, k, rows):
            c.wait()
        h, x, y = rows // 2, self.x, self.y
        a, b = slice(0, h), slice(h, rows)
        sx, rx, s2, r2 = (lax.rem(k, m) for m in (SX, RX, S2, R2))
        if n == 1:
            for i in range(2):
                self.sx[sx, i, a, :] = self.chip(k, 1 - x, i, a).astype(BF)
                self.sy[sx, i, a, :] = self.chip(k, i, 1 - y, b).astype(BF)
        elif n == 2:
            self.s2[s2, 0, a, :] = (self.chip(k, x, 1 - y, a) + self.rx[rx, 1 - y, a, :].astype(F32)).astype(BF)
            self.s2[s2, 1, a, :] = (self.chip(k, 1 - x, y, b) + self.ry[rx, 1 - x, a, :].astype(F32)).astype(BF)
        else:
            first = self.chip(k, x, y, a) + self.rx[rx, y, a, :].astype(F32) + self.r2[r2, 0, a, :].astype(F32)
            second = self.chip(k, x, y, b) + self.ry[rx, x, a, :].astype(F32) + self.r2[r2, 1, a, :].astype(F32)
            first, second = first.astype(BF), second.astype(BF)
            self.put(k, rows, first, second)
            for g in (first, second):
                g = g.astype(F32)
                self.squares[...] += jnp.sum(g * g, 0, keepdims=True)
        if n < 3:
            self.start(n, k, rows)

    def point(self, t, middle, gu, dd):
        for n, k in ((1, t - 1), (3, t - 4)) if middle else ((0, t - 1), (2, t - 3)):
            for low, high, rows in ((0, gu, GU), (gu, gu + dd, DD)):

                @pl.when((k >= low) & (k < high))
                def _():
                    if n:
                        self.stage(n, k, rows)
                    else:
                        self.start(0, k, rows)


def exchange_scratch():
    half = (2, DD // 2, NB)
    return [
        pltpu.VMEM((SRC, 4, 2, DD, NB), BF),
        pltpu.VMEM((RC, 4, DD, NB), BF),
        pltpu.VMEM((SX, *half), BF),
        pltpu.VMEM((SX, *half), BF),
        pltpu.VMEM((RX, *half), BF),
        pltpu.VMEM((RX, *half), BF),
        pltpu.VMEM((S2, *half), BF),
        pltpu.VMEM((R2, *half), BF),
        pltpu.SemaphoreType.DMA((5, RX)),
        pltpu.SemaphoreType.DMA((5, RX)),
    ]


def backward(a, dh, h, gate, up, sq1, wg, wu, wd, layer, collective_id):
    t_, d = a.shape
    ff = wg.shape[2]
    n_gu, n_dd = ff // NB, d // NB
    last = n_gu + n_dd + 3
    inner = h is not None

    def body(*refs):
        if inner:
            a_hbm, dh_ref, h_hbm, wg_ref, wu_ref, wd_ref, rg_ref, ru_ref, rd_ref, sq_ref, o_hbm, abuf, acc, w, io, *refs = refs
        else:
            a_hbm, dh_ref, gate_ref, up_ref, wd_ref, sq1_ref, rg_ref, ru_ref, rd_ref, sum_ref, abuf, sq_ref, sums, sums_got, sums_sem, io, *refs = refs
        at, ht, dgu, *refs = refs
        src = refs[0]
        t = pl.program_id(0)

        def put(k, rows, first, second):
            if rows == GU:
                cols = pl.ds(pl.multiple_of(k * NB, NB), NB)
                rg_ref[:, cols] = first
                ru_ref[:, cols] = second
            else:
                cols = pl.ds(pl.multiple_of((k - n_gu) * NB, NB), NB)
                rd_ref[: DD // 2, cols] = first
                rd_ref[DD // 2 :, cols] = second

        ex = Exchange(*refs, sq_ref, put)

        @pl.when(t == 0)
        def _():
            ex.barrier()
            sq_ref[...] = jnp.zeros_like(sq_ref)
            load = pltpu.make_async_copy(a_hbm, abuf, io)
            load.start()
            if inner:
                for r in tiles(t_, 256):
                    acc[r, :] = jnp.zeros((256, d), F32)
            load.wait()
            for r in tiles(t_, 256):
                at[:, r] = abuf[r, :].T

        ex.point(t, False, n_gu, n_dd)
        slot = lax.rem(t, SRC)

        @pl.when(t < n_gu)
        def _():
            rows = pl.ds(pl.multiple_of(t * NB, NB), NB)
            if inner:
                beside(w, wg_ref, wu_ref)
            for r in tiles(t_, 512):
                if inner:
                    both = dot(abuf[r, :], w[...])
                    gt, u = both[:, :NB], both[:, NB:]
                else:
                    gt, u = gate_ref[r, :], up_ref[r, :]
                dp = dot(dh_ref[r, :], wd_ref[...], 1, 1).astype(BF).astype(F32)
                dgt, dut, sg = hidden_back(dp, gt, u)
                dgu[r, :NB] = dgt
                dgu[r, NB:] = dut
                ht[rows, r] = (sg * u).astype(BF).T
                if inner:
                    acc[r, :] += dot(jnp.concatenate([dgt, dut], 1), w[...], 1, 1)

        def down(i):
            cols = pl.ds(pl.multiple_of((t - n_gu) * NB, NB), NB)
            src[slot, i] = dot(ht[pl.ds(i * 2 * DD, 2 * DD), :], dh_ref[:, cols]).astype(BF).reshape(2, DD, NB)

        ex.point(t, True, n_gu, n_dd)

        @pl.when(t < n_gu)
        def _():
            for i in range(2):
                both = dot(at[pl.ds(i * d // 2, d // 2), :], dgu[...]).astype(BF)
                src[slot, 2 * i : 2 * i + 2, :, : GU // 2, :] = both[:, :NB].reshape(2, 2, GU // 2, NB)
                src[slot, 2 * i : 2 * i + 2, :, GU // 2 : GU, :] = both[:, NB:].reshape(2, 2, GU // 2, NB)

        @pl.when((t >= n_gu) & (t < n_gu + n_dd))
        def _():
            for i in range(4):
                down(i)

        if inner:

            @pl.when(t == n_gu)
            def _():
                pltpu.make_async_copy(h_hbm, abuf, io).start()

            @pl.when(t == n_gu + n_dd)
            def _():
                pltpu.make_async_copy(h_hbm, abuf, io).wait()
                for r in tiles(t_, 256):
                    da = acc[r, :].astype(BF).astype(F32)
                    wide = abuf[r, :].astype(F32)
                    scale = lax.rsqrt(jnp.mean(wide * wide, -1, keepdims=True) + 1e-6)
                    along = jnp.sum(da * wide, -1, keepdims=True) * (scale * scale * scale / d)
                    abuf[r, :] = dh_ref[r, :] + (da * scale - wide * along).astype(BF)

            @pl.when(t == n_gu + n_dd + 1)
            def _():
                pltpu.make_async_copy(abuf, o_hbm, io).start()

            @pl.when(t == last)
            def _():
                pltpu.make_async_copy(abuf, o_hbm, io).wait()

        else:

            @pl.when(t == last)
            def _():
                total = jnp.sum(sq_ref[...] + sq1_ref[...], 1, keepdims=True)
                total = jnp.broadcast_to(total, (8, 128))
                for i, other in enumerate((ex.over_c, ex.over_y, ex.over_x)):
                    sums[i] = total
                    copy = pltpu.make_async_remote_copy(
                        src_ref=sums.at[i], dst_ref=sums_got.at[i], send_sem=sums_sem.at[0, i], recv_sem=sums_sem.at[1, i],
                        device_id={"dp": other}, device_id_type=MESH,
                    )
                    copy.start()
                    copy.wait()
                    total = total + sums_got[i]
                sum_ref[...] = total

    def block(j):
        return jnp.minimum(j, n_gu - 1)

    once = pl.Buffered(1)
    anyw = pl.BlockSpec(memory_space=pl.ANY)
    dh_spec = pl.BlockSpec((t_, d), lambda j: (0, 0), pipeline_mode=once)
    wcol = pl.BlockSpec((None, d, NB), lambda j: (layer, 0, block(j)))
    wrow = pl.BlockSpec((None, NB, d), lambda j: (layer, block(j), 0))
    gcol = pl.BlockSpec((t_, NB), lambda j: (0, block(j)))
    in_specs = [anyw, dh_spec, anyw, wcol, wcol, wrow] if inner else [anyw, dh_spec, gcol, gcol, wrow, whole((1, NB))]
    args = (a, dh, h, wg, wu, wd) if inner else (a, dh, gate, up, wd, sq1)
    shapes = [(d // 8, ff), (d // 8, ff), (ff // 8, d)]
    sums = (1, NB) if inner else (8, 128)
    out_specs = [whole(s) for s in shapes + [sums]] + ([anyw] if inner else [])
    out_shape = [jax.ShapeDtypeStruct(s, BF) for s in shapes] + [jax.ShapeDtypeStruct(sums, F32)]
    out_shape += [jax.ShapeDtypeStruct((t_, d), BF)] if inner else []
    scratch = [pltpu.VMEM((t_, d), BF)]
    if inner:
        scratch += [pltpu.VMEM((t_, d), F32), pltpu.VMEM((d, 2 * NB), BF)]
    else:
        scratch += [pltpu.VMEM((1, NB), F32)] + [pltpu.VMEM((3, 8, 128), F32)] * 2 + [pltpu.SemaphoreType.DMA((2, 3))]
    scratch += [pltpu.SemaphoreType.DMA, pltpu.VMEM((d, t_), BF), pltpu.VMEM((ff, t_), BF), pltpu.VMEM((t_, 2 * NB), BF)]
    return pl.pallas_call(
        body,
        grid=(last + 1,),
        in_specs=in_specs,
        out_specs=out_specs,
        out_shape=out_shape,
        scratch_shapes=scratch + exchange_scratch(),
        compiler_params=pltpu.CompilerParams(
            vmem_limit_bytes=VM, dimension_semantics=("arbitrary",), collective_id=collective_id, has_side_effects=True
        ),
        cost_estimate=cost((16 if inner else 8) * t_ * d * ff, 0),
    )(*args)


def swap(bit):
    return [(i, i ^ bit) for i in range(8)]


def send(t, bit):
    return lax.ppermute(t, "dp", swap(bit))


def place(out, pieces, where, shape):
    rows, n = pieces[0].shape
    count = len(pieces)

    def body(*refs):
        pieces, (o_ref, held, sems) = refs[:count], refs[-3:]
        me = lax.axis_index("dp")
        x, y, c = me // 4, me // 2 % 2, me % 2
        loads = [pltpu.make_async_copy(p, held.at[i], sems.at[0, i]) for i, p in enumerate(pieces)]
        stores = []
        for load in loads:
            load.start()
        for i, (load, (layer, fx, fy, fc)) in enumerate(zip(loads, where)):
            block = (abs(fx - x) * 2 + abs(fy - y)) * 2 + abs(fc - c)
            at = pl.ds(pl.multiple_of(block * rows, rows), rows)
            load.wait()
            stores.append(pltpu.make_async_copy(held.at[i], o_ref.at[layer, at], sems.at[1, i]))
            stores[-1].start()
        for store in stores:
            store.wait()

    args = (*pieces, *(() if out is None else (out,)))
    return pl.pallas_call(
        body,
        in_specs=[pl.BlockSpec(memory_space=pl.ANY)] * len(args),
        out_specs=pl.BlockSpec(memory_space=pl.ANY),
        out_shape=jax.ShapeDtypeStruct(shape, BF),
        scratch_shapes=[pltpu.VMEM((count, rows, n), BF), pltpu.SemaphoreType.DMA((2, count))],
        input_output_aliases={} if out is None else {count: 0},
        cost_estimate=cost(2_000_000_000 * count, 4 * count * rows * n),
        name="place",
    )(*args)


def gathered(owns, shapes, others):
    first = [(own, send(own, 4), send(own, 2), send(own, 1)) for own in owns]
    outs, corners, before = [None] * len(shapes), [], None
    for i, (own, from_x, from_y, from_c) in enumerate(first):
        n, l = divmod(i, 2)
        if i:
            from_x, from_y, outs[before] = lax.optimization_barrier((from_x, from_y, outs[before]))
        corners.append(send(*((from_y, 4) if l else (from_x, 2))))
        pieces = own, from_c, from_x, from_y, send(from_x, 1), send(from_y, 1)
        where = (l, 0, 0, 0), (l, 0, 0, 1), (l, 1, 0, 0), (l, 0, 1, 0), (l, 1, 0, 1), (l, 0, 1, 1)
        outs[n] = place(outs[n], pieces, where, shapes[n])
        before = n
    corners[0], outs[before], *others = lax.optimization_barrier((corners[0], outs[before], *others))
    where = (0, 1, 1, 0), (1, 1, 1, 0), (0, 1, 1, 1), (1, 1, 1, 1)
    for n in range(len(outs)):
        pair = corners[2 * n : 2 * n + 2]
        if n:
            *pair, outs[n - 1] = lax.optimization_barrier((*pair, outs[n - 1]))
        pieces = *pair, *(send(t, 1) for t in pair)
        outs[n] = place(outs[n], pieces, where, shapes[n])
    return outs, others


def moments_of(m, v, g):
    return 0.9 * m + 0.1 * g, 0.95 * v + 0.05 * g * g


def weight_of(w, m, v):
    return (w - 0.02 * (m * lax.rsqrt(v + 1e-8) + 0.1 * w)).astype(BF)


def solution(mesh):
    def step(x, dy, wg, wu, wd, *moments):
        me = lax.axis_index("dp")
        x, dy = x[0], dy[0]

        gate, up, a0, h1, a1 = fwd0(x, wg, wu, wd, 0)
        r_g1, r_u1, r_d1, sq1, dh = backward(a1, dy, h1, None, None, None, wg, wu, wd, 1, 1)
        r_g0, r_u0, r_d0, total = backward(a0, dh, None, gate, up, sq1, wg, wu, wd, 0, 2)
        count = sum(w.size for w in (wg, wu, wd))
        factor = jnp.minimum(1.0, 0.5 * lax.rsqrt(total[0, 0] / count + 1e-30))
        grads = ((r_g0, r_g1), (r_u0, r_u1), (r_d0, r_d1))
        weights, m, v = (wg, wu, wd), moments[:3], moments[3:]
        owns, now = [], factor
        for n, w in enumerate(weights):
            rows = m[n].shape[1]
            for l, g in enumerate(grads[n]):
                own = lax.dynamic_slice(w, (l, me * rows, 0), (1, rows, w.shape[2]))[0]
                own = weight_of(own.astype(F32), *moments_of(m[n][l], v[n][l], g.astype(F32) * now))
                own, now = lax.optimization_barrier((own, now))
                owns.append(own)
        new = [moments_of(m[n], v[n], jnp.stack(grads[n]).astype(F32) * now) for n in range(3)]
        outs, others = gathered(owns, [w.shape for w in weights], [t for pair in zip(*new) for t in pair])
        return (*outs, *others)

    P = jax.sharding.PartitionSpec
    rows = P(None, "dp", None)
    return jax.shard_map(
        step,
        mesh=mesh,
        in_specs=(P(("rep", "dp")),) * 2 + (P(),) * 3 + (rows,) * 6,
        out_specs=(P("rep"),) * 3 + (P("rep", "dp", None),) * 6,
        check_vma=False,
    )
```

profile of v0, /device:TPU:0, one launch (start us, length us, event | category | flops | bytes accessed | tf_op | source)
XLA Modules:
  0.0 517.8 jit_solution(5863241093385903731)
XLA Ops:
  0.6 46.5 %forward0.1 = (f32[2048,2816]{1,0:T(8,128)}, f32[2048,2816]{1,0:T(8,128)}, bf16[2048,1024]{1,0:T(8,128)(2,1)}, bf16[2048,1024]{1,0:T(8,128)(2,1)}, bf16[2048,1024]{1,0:T(8,128)(2,1)}) custom-call(bf16[2048,1024]{1,0:T(8,128)(2,1)} %bitcast.69, bf16[2,1024,2816]{2,1,0:T(8,128)(2,1)} %refs_3_.1, bf16[2,1024,2816]{2,1,0:T(8,128)(2,1)} %refs_4_.2, ...), custom_call_target="tpu_custom_call" | custom-call | flops 35433480192 | tf_op jit(solution)/shard_map/forward0/pallas_call | solution.py:101
  47.1 146.2 %shard_map.178 = (bf16[128,2816]{1,0:T(8,128)(2,1)}, bf16[128,2816]{1,0:T(8,128)(2,1)}, bf16[352,1024]{1,0:T(8,128)(2,1)}, f32[1,256]{1,0:T(1,128)}, bf16[2048,1024]{1,0:T(8,128)(2,1)}) custom-call(bf16[2048,1024]{1,0:T(8,128)(2,1)} %get-tuple-element.65.refs_0_, bf16[2048,1024]{1,0:T(8,128)(2,1)} %bitcast.70, bf16[2048,1024]{1,0:T(8,128)(2,1)} %get-tuple-element.66.refs_2_, ...), custom_call_target="tpu_custom_call" | custom-call | flops 94489280512 | tf_op jit(solution)/shard_map/pallas_call | solution.py:375
  193.4 104.2 %shard_map.179 = (bf16[128,2816]{1,0:T(8,128)(2,1)}, bf16[128,2816]{1,0:T(8,128)(2,1)}, bf16[352,1024]{1,0:T(8,128)(2,1)}, f32[8,128]{1,0:T(8,128)}) custom-call(bf16[2048,1024]{1,0:T(8,128)(2,1)} %get-tuple-element.64.refs_0_, bf16[2048,1024]{1,0:T(8,128)(2,1)} %get-tuple-element.67.refs_1_, f32[2048,2816]{1,0:T(8,128)} %get-tuple-element.68.refs_2_, ...), custom_call_target="tpu_custom_call" | custom-call | flops 47244640256 | tf_op jit(solution)/shard_map/pallas_call | solution.py:375
  297.6 1.2 slice.42
  299.5 3.2 fusion.5.refs_0_
  304.8 14.6 %collective-permute-done.7.refs_3_ = bf16[128,2816]{1,0:T(8,128)(2,1)S(1)} collective-permute-done((bf16[128,2816]{1,0:T(8,128)(2,1)S(1)}, bf16[128,2816]{1,0:T(8,128)(2,1)S(1)}, u32[]{:S(2)}, u32[]{:S(2)}) %collective-permute-start.7) | collective-permute-done | bytes 720928 | tf_op jit(solution)/shard_map/ppermute | solution.py:394
  320.1 3.5 fusion.8.refs_0_
  327.4 3.6 place.9.refs_6_
  331.0 11.3 %collective-permute-done.4.refs_3_ = bf16[128,2816]{1,0:T(8,128)(2,1)} collective-permute-done((bf16[128,2816]{1,0:T(8,128)(2,1)}, bf16[128,2816]{1,0:T(8,128)(2,1)}, u32[]{:S(2)}, u32[]{:S(2)}) %collective-permute-start.4) | collective-permute-done | bytes 720928 | tf_op jit(solution)/shard_map/ppermute | solution.py:394
  343.5 3.9 fusion.11.refs_0_
  349.4 3.6 place.10.refs_4_
  353.0 13.2 %collective-permute-done.1.refs_3_ = bf16[128,2816]{1,0:T(8,128)(2,1)} collective-permute-done((bf16[128,2816]{1,0:T(8,128)(2,1)}, bf16[128,2816]{1,0:T(8,128)(2,1)}, u32[]{:S(2)}, u32[]{:S(2)}) %collective-permute-start.1) | collective-permute-done | bytes 720928 | tf_op jit(solution)/shard_map/ppermute | solution.py:394
  367.4 3.9 fusion.14.refs_0_
  373.4 3.6 place.11.refs_6_
  376.9 13.2 %collective-permute-done.14.refs_3_ = bf16[128,2816]{1,0:T(8,128)(2,1)} collective-permute-done((bf16[128,2816]{1,0:T(8,128)(2,1)}, bf16[128,2816]{1,0:T(8,128)(2,1)}, u32[]{:S(2)}, u32[]{:S(2)}) %collective-permute-start.14) | collective-permute-done | bytes 720928 | tf_op jit(solution)/shard_map/ppermute | solution.py:394
  391.5 3.9 fusion.17.refs_0_
  397.4 3.6 place.12.refs_4_
  401.0 12.7 %collective-permute-done.25.refs_3_ = bf16[352,1024]{1,0:T(8,128)(2,1)} collective-permute-done((bf16[352,1024]{1,0:T(8,128)(2,1)}, bf16[352,1024]{1,0:T(8,128)(2,1)}, u32[]{:S(2)}, u32[]{:S(2)}) %collective-permute-start.25) | collective-permute-done | bytes 720928 | tf_op jit(solution)/shard_map/ppermute | solution.py:394
  414.9 3.9 fusion.20.refs_0_
  421.9 3.6 place.13.refs_6_
  425.5 11.7 %collective-permute-done.22.refs_3_ = bf16[352,1024]{1,0:T(8,128)(2,1)} collective-permute-done((bf16[352,1024]{1,0:T(8,128)(2,1)}, bf16[352,1024]{1,0:T(8,128)(2,1)}, u32[]{:S(2)}, u32[]{:S(2)}) %collective-permute-start.22) | collective-permute-done | bytes 720928 | tf_op jit(solution)/shard_map/ppermute | solution.py:394
  437.2 2.0 collective-permute-done.21.refs_2_
  439.7 9.3 %fusion = (f32[2,128,2816]{2,1,0:T(8,128)}, f32[2,128,2816]{2,1,0:T(8,128)}, f32[2,128,2816]{2,1,0:T(8,128)}, f32[2,128,2816]{2,1,0:T(8,128)}) fusion(f32[2,128,2816]{2,1,0:T(8,128)S(1)} %copy-done, f32[]{:T(128)} %bitcast.8, bf16[1,128,2816]{2,1,0:T(8,128)(2,1)} %bitcast.63, bf16[1,128,2816]{2,1,0:T(8,128)(2,1)} %bitcast.65, f32[2,128,2816]{2,1,0:T(8,128)} %param.16, ...), kind=kLoop, calls=%fused_computation.3 | loop fusion | flops 14417920 | bytes 25952260 | tf_op jit(solution)/shard_map/add | solution.py:455
  450.1 3.5 fusion.2
  454.6 3.6 place.14.refs_4_
  458.2 13.4 %collective-permute-done.19.refs_0_ = bf16[128,2816]{1,0:T(8,128)(2,1)S(1)} collective-permute-done((bf16[128,2816]{1,0:T(8,128)(2,1)S(1)}, bf16[128,2816]{1,0:T(8,128)(2,1)S(1)}, u32[]{:S(2)}, u32[]{:S(2)}) %collective-permute-start.19) | collective-permute-done | bytes 720928 | tf_op jit(solution)/shard_map/ppermute | solution.py:394
  474.5 2.7 place.15
  477.3 13.1 %collective-permute-done.12.refs_0_ = bf16[128,2816]{1,0:T(8,128)(2,1)S(1)} collective-permute-done((bf16[128,2816]{1,0:T(8,128)(2,1)}, bf16[128,2816]{1,0:T(8,128)(2,1)S(1)}, u32[]{:S(2)}, u32[]{:S(2)}) %collective-permute-start.12) | collective-permute-done | bytes 720928 | tf_op jit(solution)/shard_map/ppermute | solution.py:394
  494.5 2.8 place.16
  497.2 12.6 %collective-permute-done.36.refs_0_ = bf16[352,1024]{1,0:T(8,128)(2,1)S(1)} collective-permute-done((bf16[352,1024]{1,0:T(8,128)(2,1)}, bf16[352,1024]{1,0:T(8,128)(2,1)S(1)}, u32[]{:S(2)}, u32[]{:S(2)}) %collective-permute-start.36) | collective-permute-done | bytes 720928 | tf_op jit(solution)/shard_map/ppermute | solution.py:394
  511.1 1.7 collective-permute-done.40.refs_2_
  514.7 2.7 place.17
  (115 shorter events, 33.4 us)
Async XLA Ops:
  302.7 16.7 %collective-permute-start.7 = (bf16[128,2816]{1,0:T(8,128)(2,1)S(1)}, bf16[128,2816]{1,0:T(8,128)(2,1)S(1)}, u32[]{:S(2)}, u32[]{:S(2)}) collective-permute-start(bf16[128,2816]{1,0:T(8,128)(2,1)S(1)} %fusion.5.refs_0_), channel_id=1, source_target_pairs={{0,2},{1,3},{2,0},{3,1},{4,6},{5,7},{6,4},{7,5}} | collective-permute-start | bytes 2162696 | tf_op jit(solution)/shard_map/ppermute | solution.py:394
  303.7 16.4 %collective-permute-start.6 = (bf16[128,2816]{1,0:T(8,128)(2,1)S(1)}, bf16[128,2816]{1,0:T(8,128)(2,1)S(1)}, u32[]{:S(2)}, u32[]{:S(2)}) collective-permute-start(bf16[128,2816]{1,0:T(8,128)(2,1)S(1)} %fusion.5.refs_0_), channel_id=1, source_target_pairs={{0,4},{1,5},{2,6},{3,7},{4,0},{5,1},{6,2},{7,3}} | collective-permute-start | bytes 2162696 | tf_op jit(solution)/shard_map/ppermute | solution.py:394
  304.8 20.9 %collective-permute-start.5 = (bf16[128,2816]{1,0:T(8,128)(2,1)S(1)}, bf16[128,2816]{1,0:T(8,128)(2,1)S(1)}, u32[]{:S(2)}, u32[]{:S(2)}) collective-permute-start(bf16[128,2816]{1,0:T(8,128)(2,1)S(1)} %fusion.5.refs_0_), channel_id=1, source_target_pairs={{0,1},{1,0},{2,3},{3,2},{4,5},{5,4},{6,7},{7,6}} | collective-permute-start | bytes 2162696 | tf_op jit(solution)/shard_map/ppermute | solution.py:394
  320.1 7.3 %collective-permute-start.8 = (bf16[128,2816]{1,0:T(8,128)(2,1)S(1)}, bf16[128,2816]{1,0:T(8,128)(2,1)}, u32[]{:S(2)}, u32[]{:S(2)}) collective-permute-start(bf16[128,2816]{1,0:T(8,128)(2,1)S(1)} %collective-permute-done.6.refs_2_), channel_id=1, source_target_pairs={{0,1},{1,0},{2,3},{3,2},{4,5},{5,4},{6,7},{7,6}} | collective-permute-start | bytes 2162696 | tf_op jit(solution)/shard_map/ppermute | solution.py:394
  323.6 18.6 %collective-permute-start.4 = (bf16[128,2816]{1,0:T(8,128)(2,1)}, bf16[128,2816]{1,0:T(8,128)(2,1)}, u32[]{:S(2)}, u32[]{:S(2)}) collective-permute-start(bf16[128,2816]{1,0:T(8,128)(2,1)} %fusion.8.refs_0_), channel_id=1, source_target_pairs={{0,2},{1,3},{2,0},{3,1},{4,6},{5,7},{6,4},{7,5}} | collective-permute-start | bytes 2162696 | tf_op jit(solution)/shard_map/ppermute | solution.py:394
  324.7 18.3 %collective-permute-start.3 = (bf16[128,2816]{1,0:T(8,128)(2,1)}, bf16[128,2816]{1,0:T(8,128)(2,1)}, u32[]{:S(2)}, u32[]{:S(2)}) collective-permute-start(bf16[128,2816]{1,0:T(8,128)(2,1)} %fusion.8.refs_0_), channel_id=1, source_target_pairs={{0,4},{1,5},{2,6},{3,7},{4,0},{5,1},{6,2},{7,3}} | collective-permute-start | bytes 2162696 | tf_op jit(solution)/shard_map/ppermute | solution.py:394
  325.6 22.7 %collective-permute-start.2 = (bf16[128,2816]{1,0:T(8,128)(2,1)}, bf16[128,2816]{1,0:T(8,128)(2,1)}, u32[]{:S(2)}, u32[]{:S(2)}) collective-permute-start(bf16[128,2816]{1,0:T(8,128)(2,1)} %fusion.8.refs_0_), channel_id=1, source_target_pairs={{0,1},{1,0},{2,3},{3,2},{4,5},{5,4},{6,7},{7,6}} | collective-permute-start | bytes 2162696 | tf_op jit(solution)/shard_map/ppermute | solution.py:394
  347.4 25.0 %collective-permute-start.15 = (bf16[128,2816]{1,0:T(8,128)(2,1)}, bf16[128,2816]{1,0:T(8,128)(2,1)}, u32[]{:S(2)}, u32[]{:S(2)}) collective-permute-start(bf16[128,2816]{1,0:T(8,128)(2,1)} %fusion.11.refs_0_), channel_id=1, source_target_pairs={{0,1},{1,0},{2,3},{3,2},{4,5},{5,4},{6,7},{7,6}} | collective-permute-start | bytes 2162696 | tf_op jit(solution)/shard_map/ppermute | solution.py:394
  347.4 18.9 %collective-permute-start.1 = (bf16[128,2816]{1,0:T(8,128)(2,1)}, bf16[128,2816]{1,0:T(8,128)(2,1)}, u32[]{:S(2)}, u32[]{:S(2)}) collective-permute-start(bf16[128,2816]{1,0:T(8,128)(2,1)} %fusion.11.refs_0_), channel_id=1, source_target_pairs={{0,2},{1,3},{2,0},{3,1},{4,6},{5,7},{6,4},{7,5}} | collective-permute-start | bytes 2162696 | tf_op jit(solution)/shard_map/ppermute | solution.py:394
  348.3 18.6 %collective-permute-start = (bf16[128,2816]{1,0:T(8,128)(2,1)}, bf16[128,2816]{1,0:T(8,128)(2,1)}, u32[]{:S(2)}, u32[]{:S(2)}) collective-permute-start(bf16[128,2816]{1,0:T(8,128)(2,1)} %fusion.11.refs_0_), channel_id=1, source_target_pairs={{0,4},{1,5},{2,6},{3,7},{4,0},{5,1},{6,2},{7,3}} | collective-permute-start | bytes 2162696 | tf_op jit(solution)/shard_map/ppermute | solution.py:394
  371.3 26.1 %collective-permute-start.26 = (bf16[128,2816]{1,0:T(8,128)(2,1)}, bf16[128,2816]{1,0:T(8,128)(2,1)}, u32[]{:S(2)}, u32[]{:S(2)}) collective-permute-start(bf16[128,2816]{1,0:T(8,128)(2,1)} %fusion.14.refs_0_), channel_id=1, source_target_pairs={{0,1},{1,0},{2,3},{3,2},{4,5},{5,4},{6,7},{7,6}} | collective-permute-start | bytes 2162696 | tf_op jit(solution)/shard_map/ppermute | solution.py:394
  371.3 18.9 %collective-permute-start.14 = (bf16[128,2816]{1,0:T(8,128)(2,1)}, bf16[128,2816]{1,0:T(8,128)(2,1)}, u32[]{:S(2)}, u32[]{:S(2)}) collective-permute-start(bf16[128,2816]{1,0:T(8,128)(2,1)} %fusion.14.refs_0_), channel_id=1, source_target_pairs={{0,2},{1,3},{2,0},{3,1},{4,6},{5,7},{6,4},{7,5}} | collective-permute-start | bytes 2162696 | tf_op jit(solution)/shard_map/ppermute | solution.py:394
  372.4 18.6 %collective-permute-start.13 = (bf16[128,2816]{1,0:T(8,128)(2,1)}, bf16[128,2816]{1,0:T(8,128)(2,1)}, u32[]{:S(2)}, u32[]{:S(2)}) collective-permute-start(bf16[128,2816]{1,0:T(8,128)(2,1)} %fusion.14.refs_0_), channel_id=1, source_target_pairs={{0,4},{1,5},{2,6},{3,7},{4,0},{5,1},{6,2},{7,3}} | collective-permute-start | bytes 2162696 | tf_op jit(solution)/shard_map/ppermute | solution.py:394
  391.0 6.4 %collective-permute-start.27 = (bf16[128,2816]{1,0:T(8,128)(2,1)}, bf16[128,2816]{1,0:T(8,128)(2,1)}, u32[]{:S(2)}, u32[]{:S(2)}) collective-permute-start(bf16[128,2816]{1,0:T(8,128)(2,1)} %collective-permute-done.13.refs_2_), channel_id=1, source_target_pairs={{0,1},{1,0},{2,3},{3,2},{4,5},{5,4},{6,7},{7,6}} | collective-permute-start | bytes 2162696 | tf_op jit(solution)/shard_map/ppermute | solution.py:394
  391.0 6.4 %collective-permute-start.28 = (bf16[128,2816]{1,0:T(8,128)(2,1)}, bf16[128,2816]{1,0:T(8,128)(2,1)}, u32[]{:S(2)}, u32[]{:S(2)}) collective-permute-start(bf16[128,2816]{1,0:T(8,128)(2,1)} %collective-permute-done.14.refs_3_), channel_id=1, source_target_pairs={{0,1},{1,0},{2,3},{3,2},{4,5},{5,4},{6,7},{7,6}} | collective-permute-start | bytes 2162696 | tf_op jit(solution)/shard_map/ppermute | solution.py:394
  395.4 18.4 %collective-permute-start.25 = (bf16[352,1024]{1,0:T(8,128)(2,1)}, bf16[352,1024]{1,0:T(8,128)(2,1)}, u32[]{:S(2)}, u32[]{:S(2)}) collective-permute-start(bf16[352,1024]{1,0:T(8,128)(2,1)} %fusion.17.refs_0_), channel_id=1, source_target_pairs={{0,2},{1,3},{2,0},{3,1},{4,6},{5,7},{6,4},{7,5}} | collective-permute-start | bytes 2162696 | tf_op jit(solution)/shard_map/ppermute | solution.py:394
  396.3 18.1 %collective-permute-start.24 = (bf16[352,1024]{1,0:T(8,128)(2,1)}, bf16[352,1024]{1,0:T(8,128)(2,1)}, u32[]{:S(2)}, u32[]{:S(2)}) collective-permute-start(bf16[352,1024]{1,0:T(8,128)(2,1)} %fusion.17.refs_0_), channel_id=1, source_target_pairs={{0,4},{1,5},{2,6},{3,7},{4,0},{5,1},{6,2},{7,3}} | collective-permute-start | bytes 2162696 | tf_op jit(solution)/shard_map/ppermute | solution.py:394
  397.4 23.4 %collective-permute-start.23 = (bf16[352,1024]{1,0:T(8,128)(2,1)}, bf16[352,1024]{1,0:T(8,128)(2,1)}, u32[]{:S(2)}, u32[]{:S(2)}) collective-permute-start(bf16[352,1024]{1,0:T(8,128)(2,1)} %fusion.17.refs_0_), channel_id=1, source_target_pairs={{0,1},{1,0},{2,3},{3,2},{4,5},{5,4},{6,7},{7,6}} | collective-permute-start | bytes 2162696 | tf_op jit(solution)/shard_map/ppermute | solution.py:394
  414.4 6.4 %collective-permute-start.30 = (bf16[352,1024]{1,0:T(8,128)(2,1)}, bf16[352,1024]{1,0:T(8,128)(2,1)}, u32[]{:S(2)}, u32[]{:S(2)}) collective-permute-start(bf16[352,1024]{1,0:T(8,128)(2,1)} %collective-permute-done.25.refs_3_), channel_id=1, source_target_pairs={{0,1},{1,0},{2,3},{3,2},{4,5},{5,4},{6,7},{7,6}} | collective-permute-start | bytes 2162696 | tf_op jit(solution)/shard_map/ppermute | solution.py:394
  414.4 7.5 %collective-permute-start.29 = (bf16[352,1024]{1,0:T(8,128)(2,1)}, bf16[352,1024]{1,0:T(8,128)(2,1)}, u32[]{:S(2)}, u32[]{:S(2)}) collective-permute-start(bf16[352,1024]{1,0:T(8,128)(2,1)} %collective-permute-done.24.refs_2_), channel_id=1, source_target_pairs={{0,1},{1,0},{2,3},{3,2},{4,5},{5,4},{6,7},{7,6}} | collective-permute-start | bytes 2162696 | tf_op jit(solution)/shard_map/ppermute | solution.py:394
  418.8 18.4 %collective-permute-start.22 = (bf16[352,1024]{1,0:T(8,128)(2,1)}, bf16[352,1024]{1,0:T(8,128)(2,1)}, u32[]{:S(2)}, u32[]{:S(2)}) collective-permute-start(bf16[352,1024]{1,0:T(8,128)(2,1)} %fusion.20.refs_0_), channel_id=1, source_target_pairs={{0,2},{1,3},{2,0},{3,1},{4,6},{5,7},{6,4},{7,5}} | collective-permute-start | bytes 2162696 | tf_op jit(solution)/shard_map/ppermute | solution.py:394
  419.9 19.3 %collective-permute-start.21 = (bf16[352,1024]{1,0:T(8,128)(2,1)}, bf16[352,1024]{1,0:T(8,128)(2,1)}, u32[]{:S(2)}, u32[]{:S(2)}) collective-permute-start(bf16[352,1024]{1,0:T(8,128)(2,1)} %fusion.20.refs_0_), channel_id=1, source_target_pairs={{0,4},{1,5},{2,6},{3,7},{4,0},{5,1},{6,2},{7,3}} | collective-permute-start | bytes 2162696 | tf_op jit(solution)/shard_map/ppermute | solution.py:394
  420.8 33.7 %collective-permute-start.20 = (bf16[352,1024]{1,0:T(8,128)(2,1)}, bf16[352,1024]{1,0:T(8,128)(2,1)}, u32[]{:S(2)}, u32[]{:S(2)}) collective-permute-start(bf16[352,1024]{1,0:T(8,128)(2,1)} %fusion.20.refs_0_), channel_id=1, source_target_pairs={{0,1},{1,0},{2,3},{3,2},{4,5},{5,4},{6,7},{7,6}} | collective-permute-start | bytes 2162696 | tf_op jit(solution)/shard_map/ppermute | solution.py:394
  420.9 33.7 %collective-permute-start.33 = (bf16[128,2816]{1,0:T(8,128)(2,1)}, bf16[128,2816]{1,0:T(8,128)(2,1)}, u32[]{:S(2)}, u32[]{:S(2)}) collective-permute-start(bf16[128,2816]{1,0:T(8,128)(2,1)} %collective-permute-done.4.refs_3_), channel_id=1, source_target_pairs={{0,4},{1,5},{2,6},{3,7},{4,0},{5,1},{6,2},{7,3}} | collective-permute-start | bytes 2162696 | tf_op jit(solution)/shard_map/ppermute | solution.py:394
  439.2 15.3 %collective-permute-start.31 = (bf16[352,1024]{1,0:T(8,128)(2,1)}, bf16[352,1024]{1,0:T(8,128)(2,1)}, u32[]{:S(2)}, u32[]{:S(2)}) collective-permute-start(bf16[352,1024]{1,0:T(8,128)(2,1)} %collective-permute-done.21.refs_2_), channel_id=1, source_target_pairs={{0,1},{1,0},{2,3},{3,2},{4,5},{5,4},{6,7},{7,6}} | collective-permute-start | bytes 2162696 | tf_op jit(solution)/shard_map/ppermute | solution.py:394
  439.2 15.3 %collective-permute-start.32 = (bf16[352,1024]{1,0:T(8,128)(2,1)}, bf16[352,1024]{1,0:T(8,128)(2,1)}, u32[]{:S(2)}, u32[]{:S(2)}) collective-permute-start(bf16[352,1024]{1,0:T(8,128)(2,1)} %collective-permute-done.22.refs_3_), channel_id=1, source_target_pairs={{0,1},{1,0},{2,3},{3,2},{4,5},{5,4},{6,7},{7,6}} | collective-permute-start | bytes 2162696 | tf_op jit(solution)/shard_map/ppermute | solution.py:394
  453.5 18.0 %collective-permute-start.19 = (bf16[128,2816]{1,0:T(8,128)(2,1)S(1)}, bf16[128,2816]{1,0:T(8,128)(2,1)S(1)}, u32[]{:S(2)}, u32[]{:S(2)}) collective-permute-start(bf16[128,2816]{1,0:T(8,128)(2,1)S(1)} %copy-done.8), channel_id=1, source_target_pairs={{0,2},{1,3},{2,0},{3,1},{4,6},{5,7},{6,4},{7,5}} | collective-permute-start | bytes 2162696 | tf_op jit(solution)/shard_map/ppermute | solution.py:394
  454.5 19.1 %collective-permute-start.35 = (bf16[128,2816]{1,0:T(8,128)(2,1)}, bf16[128,2816]{1,0:T(8,128)(2,1)S(1)}, u32[]{:S(2)}, u32[]{:S(2)}) collective-permute-start(bf16[128,2816]{1,0:T(8,128)(2,1)} %collective-permute-done.33.refs_1_), channel_id=1, source_target_pairs={{0,1},{1,0},{2,3},{3,2},{4,5},{5,4},{6,7},{7,6}} | collective-permute-start | bytes 2162696 | tf_op jit(solution)/shard_map/ppermute | solution.py:394
  471.6 18.8 %collective-permute-start.12 = (bf16[128,2816]{1,0:T(8,128)(2,1)}, bf16[128,2816]{1,0:T(8,128)(2,1)S(1)}, u32[]{:S(2)}, u32[]{:S(2)}) collective-permute-start(bf16[128,2816]{1,0:T(8,128)(2,1)} %collective-permute-done.refs_2_), channel_id=1, source_target_pairs={{0,2},{1,3},{2,0},{3,1},{4,6},{5,7},{6,4},{7,5}} | collective-permute-start | bytes 2162696 | tf_op jit(solution)/shard_map/ppermute | solution.py:394
  472.6 18.5 %collective-permute-start.18 = (bf16[128,2816]{1,0:T(8,128)(2,1)}, bf16[128,2816]{1,0:T(8,128)(2,1)S(1)}, u32[]{:S(2)}, u32[]{:S(2)}) collective-permute-start(bf16[128,2816]{1,0:T(8,128)(2,1)} %collective-permute-done.14.refs_3_), channel_id=1, source_target_pairs={{0,4},{1,5},{2,6},{3,7},{4,0},{5,1},{6,2},{7,3}} | collective-permute-start | bytes 2162696 | tf_op jit(solution)/shard_map/ppermute | solution.py:394
  491.6 18.3 %collective-permute-start.36 = (bf16[352,1024]{1,0:T(8,128)(2,1)}, bf16[352,1024]{1,0:T(8,128)(2,1)S(1)}, u32[]{:S(2)}, u32[]{:S(2)}) collective-permute-start(bf16[352,1024]{1,0:T(8,128)(2,1)} %collective-permute-done.24.refs_2_), channel_id=1, source_target_pairs={{0,2},{1,3},{2,0},{3,1},{4,6},{5,7},{6,4},{7,5}} | collective-permute-start | bytes 2162696 | tf_op jit(solution)/shard_map/ppermute | solution.py:394
  492.6 18.0 %collective-permute-start.37 = (bf16[352,1024]{1,0:T(8,128)(2,1)}, bf16[352,1024]{1,0:T(8,128)(2,1)S(1)}, u32[]{:S(2)}, u32[]{:S(2)}) collective-permute-start(bf16[352,1024]{1,0:T(8,128)(2,1)} %collective-permute-done.22.refs_3_), channel_id=1, source_target_pairs={{0,4},{1,5},{2,6},{3,7},{4,0},{5,1},{6,2},{7,3}} | collective-permute-start | bytes 2162696 | tf_op jit(solution)/shard_map/ppermute | solution.py:394
  (31 other events, 180.3 us)
where the time goes:
time: 522 us; the launch traced here: 518 us
  Pallas kernels  327 us (63%)
  waiting for transfers between devices  126 us (24%)
  other arithmetic  35 us (7%)
  starting transfers between devices  21.9 us (4%)
  local copies, waits for them, and re-layouts  6.27 us (1%)
    pallas_call x2, Pallas kernels, backward(): pl.pallas_call(body, grid=(last + 1,), in_specs=in_specs, out_specs=out_s...  250 us
    ppermute x42, waiting for transfers between devices, send(): return lax.ppermute(t, 'dp', swap(bit))  126 us
    pallas_call x1, Pallas kernels, fwd0(): pl.pallas_call(body, grid=(n1 + n2,), in_specs=[anyw, wcol, wcol, anyw],...  46.5 us
    pallas_call x9, Pallas kernels, place(): pl.pallas_call(body, in_specs=[pl.BlockSpec(memory_space=pl.ANY)] * len(a...  29.8 us
    convert_element_type x6, other arithmetic, weight_of(): return (w - 0.02 * (m * lax.rsqrt(v + 1e-08) + 0.1 * w)).astype(BF)  22.2 us
    ppermute x42, starting transfers between devices, send(): return lax.ppermute(t, 'dp', swap(bit))  21.9 us
    add x2, other arithmetic, moments_of(): return (0.9 * m + 0.1 * g, 0.95 * v + 0.05 * g * g)  12.8 us
  transfers between devices with their start and end apart: 42, of which 20 were waited for; matrix products, arithmetic and copies ran while one was open for 6% of the time, Pallas kernels for 5%

commit v1 on v0

v1 whole, which is shorter than its diff:
```python
import jax
import jax.numpy as jnp
from jax import lax
from jax.experimental import pallas as pl
from jax.experimental.pallas import tpu as pltpu


BF, F32 = jnp.bfloat16, jnp.float32
NB = 256
VM = 64 * 1024 * 1024 - 65536


def dot(a, b, ca=1, cb=0):
    return lax.dot_general(a, b, (((ca,), (cb,)), ((), ())), preferred_element_type=F32)


def normed(h):
    wide = h.astype(F32)
    scale = lax.rsqrt(jnp.mean(wide * wide, -1, keepdims=True) + 1e-6)
    return (wide * scale).astype(BF)


def params():
    return pltpu.CompilerParams(vmem_limit_bytes=VM, dimension_semantics=("arbitrary",))


def whole(shape):
    return pl.BlockSpec(shape, lambda j: (0,) * len(shape))


def cost(mm, by):
    return pl.CostEstimate(flops=mm, bytes_accessed=by, transcendentals=0)


def tiles(t, rt):
    return [pl.ds(i * rt, rt) for i in range(t // rt)]


def beside(ref, one, other):
    n = one.shape[1]
    ref[:, :n] = one[...]
    ref[:, n:] = other[...]


def forward(x, wg, wu, wd):
    t_, d = x.shape
    ff = wg.shape[2]
    n1, rt = ff // NB, 512
    n2 = t_ // rt

    def body(x_hbm, wg_ref, wu_ref, wd_hbm, gate_ref, up_ref, ht_ref, at_hbm, h_ref, xs, a, at, hid, w, wds, sem, wd_sem, at_sem):
        t = pl.program_id(0)
        second = t >= n1 + n2
        wd_load = pltpu.make_async_copy(wd_hbm.at[0], wds, wd_sem)
        early = pl.ds(0, t_ - 256)
        late = pl.ds(t_ - 256, 256)
        at_stores = [pltpu.make_async_copy(at, at_hbm.at[0], at_sem.at[0])]
        at_stores += [pltpu.make_async_copy(at.at[:, c], at_hbm.at[1, :, c], at_sem.at[i]) for i, c in enumerate((early, late))]

        @pl.when(t == 0)
        def _():
            loads = [pltpu.make_async_copy(x_hbm.at[r], xs.at[r], sem.at[i]) for i, r in enumerate(tiles(t_, rt))]
            for load in loads:
                load.start()
            wd_load.start()
            for i, load in enumerate(loads):
                load.wait()
                for r in range(i * rt, (i + 1) * rt, 256):
                    a[pl.ds(r, 256), :] = normed(xs[pl.ds(r, 256), :])

        @pl.when((t < n1) | second)
        def _():
            beside(w, wg_ref, wu_ref)
            j = jnp.where(second, t - n1 - n2, t)
            cols = pl.ds(pl.multiple_of(j * NB, NB), NB)
            part = pl.ds(pl.multiple_of(jnp.minimum(j, t_ // 256 - 1) * 256, 256), 256)
            at[:, part] = a[part, :].T
            for r in tiles(t_, rt):
                both = dot(a[r, :], w[...])
                gate, up = both[:, :NB], both[:, NB:]
                gate_ref[r, :] = gate
                up_ref[r, :] = up
                hidden = (jax.nn.silu(gate) * up).astype(BF)
                hid[r, cols] = hidden
                ht_ref[:, r] = hidden.T

        @pl.when(t == n1)
        def _():
            wd_load.wait()
            at_stores[0].start()

        @pl.when((t >= n1) & (t < n1 + n2))
        def _():
            r = pl.ds(pl.multiple_of((t - n1) * rt, rt), rt)
            h = xs[r, :] + dot(hid[r, :], wds[...]).astype(BF)
            h_ref[...] = h
            a[r, :] = normed(h)

        @pl.when(t == n1 + n2 - 1)
        def _():
            at_stores[0].wait()

        @pl.when(t == 2 * n1 + n2 - 2)
        def _():
            at_stores[1].start()

        @pl.when(t == 2 * n1 + n2 - 1)
        def _():
            at_stores[2].start()
            at_stores[1].wait()
            at_stores[2].wait()

    def layer(j):
        return jnp.where(j < n1 + n2, 0, 1)

    def block(j):
        return jnp.where(j < n1 + n2, jnp.minimum(j, n1 - 1), j - n1 - n2)

    anyw = pl.BlockSpec(memory_space=pl.ANY)
    wcol = pl.BlockSpec((None, d, NB), lambda j: (layer(j), 0, block(j)))
    gcol = pl.BlockSpec((None, t_, NB), lambda j: (layer(j), 0, block(j)))
    hrow = pl.BlockSpec((None, NB, t_), lambda j: (layer(j), block(j), 0))
    return pl.pallas_call(
        body,
        grid=(2 * n1 + n2,),
        in_specs=[anyw, wcol, wcol, anyw],
        out_specs=[gcol, gcol, hrow, anyw, pl.BlockSpec((rt, d), lambda j: (jnp.clip(j - n1, 0, n2 - 1), 0))],
        out_shape=[
            jax.ShapeDtypeStruct((2, t_, ff), F32),
            jax.ShapeDtypeStruct((2, t_, ff), F32),
            jax.ShapeDtypeStruct((2, ff, t_), BF),
            jax.ShapeDtypeStruct((2, d, t_), BF),
            jax.ShapeDtypeStruct((t_, d), BF),
        ],
        scratch_shapes=[
            pltpu.VMEM((t_, d), BF),
            pltpu.VMEM((t_, d), BF),
            pltpu.VMEM((d, t_), BF),
            pltpu.VMEM((t_, ff), BF),
            pltpu.VMEM((d, 2 * NB), BF),
            pltpu.VMEM((ff, d), BF),
            pltpu.SemaphoreType.DMA((n2,)),
            pltpu.SemaphoreType.DMA,
            pltpu.SemaphoreType.DMA((2,)),
        ],
        compiler_params=params(),
        cost_estimate=cost(10 * t_ * d * ff, 0),
        name="forward",
    )(x, wg, wu, wd)


def hidden_back(dh, gate, up):
    s = jax.nn.sigmoid(gate)
    sg = gate * s
    return (dh * up * (s + sg * (1 - s))).astype(BF), (dh * sg).astype(BF)


SLOTS = {True: (4, 5, 2, 6, 2, 4), False: (3, 3, 1, 3, 1, 2)}
MESH = pl.DeviceIdType.MESH
GU, DD = 256, 352


class Exchange:
    def __init__(self, rows, slots, squares, put, src, rc, sx, sy, rx, ry, s2, r2, sent, got):
        self.rows, self.slots = rows, slots
        self.src, self.rc, self.sx, self.sy, self.rx, self.ry, self.s2, self.r2 = src, rc, sx, sy, rx, ry, s2, r2
        self.sent, self.got, self.squares, self.put = sent, got, squares, put
        me = lax.axis_index("dp")
        self.x, self.y, self.c = me // 4, me // 2 % 2, me % 2
        self.over_c, self.over_y, self.over_x = me + 1 - 2 * self.c, me + 2 - 4 * self.y, me + 4 - 8 * self.x

    def barrier(self):
        b = pltpu.get_barrier_semaphore()
        for other in (self.over_c, self.over_y, self.over_x):
            pl.semaphore_signal(b, inc=1, device_id={"dp": other}, device_id_type=MESH)
        pl.semaphore_wait(b, 3)

    def copy(self, n, slot, src, dst, other):
        return pltpu.make_async_remote_copy(
            src_ref=src, dst_ref=dst, send_sem=self.sent.at[n, slot], recv_sem=self.got.at[n, slot],
            device_id={"dp": other}, device_id_type=MESH,
        )

    def copies(self, stage, k):
        rows, h = self.rows, self.rows // 2
        SRC, RC, SX, RX, S2, R2 = self.slots
        if stage == 0:
            s, r = lax.rem(k, SRC), lax.rem(k, RC)
            return [self.copy(0, r, self.src.at[s, :, 1 - self.c, :rows], self.rc.at[r, :, :rows], self.over_c)]
        if stage == 1:
            s, r = lax.rem(k, SX), lax.rem(k, RX)
            return [
                self.copy(1, r, self.sx.at[s, :, :h], self.rx.at[r, :, :h], self.over_x),
                self.copy(2, r, self.sy.at[s, :, :h], self.ry.at[r, :, :h], self.over_y),
            ]
        s, r = lax.rem(k, S2), lax.rem(k, R2)
        return [
            self.copy(3, r, self.s2.at[s, 0, :h], self.r2.at[r, 0, :h], self.over_y),
            self.copy(4, r, self.s2.at[s, 1, :h], self.r2.at[r, 1, :h], self.over_x),
        ]

    def start(self, stage, k):
        for c in self.copies(stage, k):
            c.start()

    def chip(self, k, i, j, part):
        at = i * 2 + j
        return self.src[lax.rem(k, self.slots[0]), at, self.c, part, :].astype(F32) + self.rc[lax.rem(k, self.slots[1]), at, part, :].astype(F32)

    def stage(self, n, k):
        for c in self.copies(n - 1, k):
            c.wait()
        rows, h, x, y = self.rows, self.rows // 2, self.x, self.y
        a, b = slice(0, h), slice(h, rows)
        sx, rx, s2, r2 = (lax.rem(k, m) for m in self.slots[2:])
        if n == 1:
            for i in range(2):
                self.sx[sx, i, a, :] = self.chip(k, 1 - x, i, a).astype(BF)
                self.sy[sx, i, a, :] = self.chip(k, i, 1 - y, b).astype(BF)
        elif n == 2:
            self.s2[s2, 0, a, :] = (self.chip(k, x, 1 - y, a) + self.rx[rx, 1 - y, a, :].astype(F32)).astype(BF)
            self.s2[s2, 1, a, :] = (self.chip(k, 1 - x, y, b) + self.ry[rx, 1 - x, a, :].astype(F32)).astype(BF)
        else:
            first = self.chip(k, x, y, a) + self.rx[rx, y, a, :].astype(F32) + self.r2[r2, 0, a, :].astype(F32)
            second = self.chip(k, x, y, b) + self.ry[rx, x, a, :].astype(F32) + self.r2[r2, 1, a, :].astype(F32)
            first, second = first.astype(BF), second.astype(BF)
            self.put(k, first, second)
            for g in (first, second):
                g = g.astype(F32)
                self.squares[...] += jnp.sum(g * g, 0, keepdims=True)
        if n < 3:
            self.start(n, k)

    def due(self, n, k, when):
        @pl.when(when)
        def _():
            if n:
                self.stage(n, k)
            else:
                self.start(0, k)


def exchange_scratch(rows, slots):
    half = (2, rows // 2, NB)
    SRC, RC, SX, RX, S2, R2 = slots
    shapes = [(SRC, 4, 2, rows, NB), (RC, 4, rows, NB), (SX, *half), (SX, *half), (RX, *half), (RX, *half), (S2, *half), (R2, *half)]
    return [pltpu.VMEM(shape, BF) for shape in shapes] + [pltpu.SemaphoreType.DMA((5, max(slots)))] * 2


def backward(at, dy, h, gate, up, ht, wg, wu, wd):
    _, d, t_ = at.shape
    ff = wg.shape[2]
    n, n_dd = ff // NB, d // NB
    last = 2 * n + 3
    skip = (n + 1) // 2 - n_dd

    def body(
        at_hbm, dy_hbm, h_hbm, g_hbm, u_hbm, ht_hbm, wg_ref, wu_ref, wd_ref, rg_ref, ru_ref, rd_ref, sum_ref,
        dh, hs, acc, w, at, gu, hbuf, dgu, sq, sums, sums_got, sums_sem, at_sem, dh_sem, h_sem, gu_sem, ht_sem, *refs,
    ):
        src, src_d = refs[0], refs[10]
        t = pl.program_id(0)
        inner = t < n

        def put_gu(k, first, second):
            rg_ref[...] = first
            ru_ref[...] = second

        def put_d(k, first, second):
            rd_ref[: DD // 2, :] = first
            rd_ref[DD // 2 :, :] = second

        ex = Exchange(GU, SLOTS[True], sq, put_gu, *refs[:10])
        ex_d = Exchange(DD, SLOTS[False], sq, put_d, *refs[10:])
        at_loads = [pltpu.make_async_copy(at_hbm.at[layer], at, at_sem) for layer in range(2)]
        dh_load = pltpu.make_async_copy(dy_hbm, dh, dh_sem)
        h_load = pltpu.make_async_copy(h_hbm, hs, h_sem)

        def gu_loads(j):
            cols = pl.ds(pl.multiple_of(lax.rem(j, n) * NB, NB), NB)
            return [pltpu.make_async_copy(r.at[1 - j // n, :, cols], gu.at[i], gu_sem.at[i]) for i, r in enumerate((g_hbm, u_hbm))]

        def ht_load():
            rows = pl.ds(pl.multiple_of(lax.rem(t, 2) * 4 * DD, 4 * DD), 4 * DD)
            return pltpu.make_async_copy(ht_hbm.at[1 - t // n, rows], hbuf, ht_sem)

        @pl.when(t == 0)
        def _():
            dh_load.start()
            for load in gu_loads(0):
                load.start()
            at_loads[1].start()
            sq[...] = jnp.zeros_like(sq)
            for r in tiles(t_, 256):
                acc[r, :] = jnp.zeros((256, d), F32)
            ex.barrier()
            dh_load.wait()

        pair, even = t // 2, lax.rem(t, 2) == 0
        odd = lax.rem(t, 2) == 1
        start = 2 * (n_dd + skip)
        making_d = (t < 2 * n_dd) | ((t >= start) & (t < start + 2 * n_dd))
        column = jnp.where(t < start, pair, pair - n_dd - skip)

        @pl.when(making_d)
        def _():
            ht_load().start()

        def due_d(stage, later, when):
            k = pair - later
            ex_d.due(stage, k, when & (k >= 0) & (k < n_dd))
            ex_d.due(stage, k - skip, when & (k >= n_dd + skip) & (k < 2 * n_dd + skip))

        ex.due(0, t - 1, (t >= 1) & (t <= 2 * n))
        due_d(0, 1, even)
        ex.due(2, t - 3, (t >= 3) & (t <= 2 * n + 2))
        due_d(2, 2, even)

        @pl.when(t == n)
        def _():
            at_loads[0].start()
            h_load.wait()
            for r in tiles(t_, 256):
                da = acc[r, :].astype(BF).astype(F32)
                wide = hs[r, :].astype(F32)
                scale = lax.rsqrt(jnp.mean(wide * wide, -1, keepdims=True) + 1e-6)
                along = jnp.sum(da * wide, -1, keepdims=True) * (scale * scale * scale / d)
                dh[r, :] = dh[r, :] + (da * scale - wide * along).astype(BF)

        def hidden_units(inner):
            for load in gu_loads(t):
                load.wait()
            if inner:
                beside(w, wg_ref, wu_ref)
            for r in tiles(t_, 512):
                dp = dot(dh[r, :], wd_ref[...], 1, 1).astype(BF).astype(F32)
                dgt, dut = hidden_back(dp, gu[0, r, :], gu[1, r, :])
                dgu[r, :NB] = dgt
                dgu[r, NB:] = dut
                if inner:
                    acc[r, :] += dot(jnp.concatenate([dgt, dut], 1), w[...], 1, 1)

        @pl.when(inner)
        def _():
            hidden_units(True)

        @pl.when((t >= n) & (t < 2 * n))
        def _():
            hidden_units(False)

        @pl.when(t < 2 * n - 1)
        def _():
            for load in gu_loads(t + 1):
                load.start()

        ex.due(1, t - 1, (t >= 1) & (t <= 2 * n))
        due_d(1, 1, even)
        ex.due(3, t - 4, (t >= 4) & (t <= 2 * n + 3))
        due_d(3, 2, odd)

        @pl.when(t == 0)
        def _():
            h_load.start()
            at_loads[1].wait()

        @pl.when(t == n)
        def _():
            at_loads[0].wait()

        @pl.when(t < 2 * n)
        def _():
            slot = lax.rem(t, SLOTS[True][0])
            for i in range(2):
                both = dot(at[pl.ds(i * d // 2, d // 2), :], dgu[...]).astype(BF)
                src[slot, 2 * i : 2 * i + 2, :, : GU // 2, :] = both[:, :NB].reshape(2, 2, GU // 2, NB)
                src[slot, 2 * i : 2 * i + 2, :, GU // 2 :, :] = both[:, NB:].reshape(2, 2, GU // 2, NB)

        @pl.when(making_d)
        def _():
            ht_load().wait()
            slot = lax.rem(jnp.where(t < start, pair, pair - skip), SLOTS[False][0])
            cols = pl.ds(pl.multiple_of(column * NB, NB), NB)
            for i in range(2):
                rows = pl.ds(i * 2 * DD, 2 * DD)
                src_d[slot, 2 * lax.rem(t, 2) + i] = dot(hbuf[rows, :], dh[:, cols]).astype(BF).reshape(2, DD, NB)

        @pl.when(t == last)
        def _():
            total = jnp.broadcast_to(jnp.sum(sq[...], 1, keepdims=True), (8, 128))
            for i, other in enumerate((ex.over_c, ex.over_y, ex.over_x)):
                sums[i] = total
                copy = pltpu.make_async_remote_copy(
                    src_ref=sums.at[i], dst_ref=sums_got.at[i], send_sem=sums_sem.at[0, i], recv_sem=sums_sem.at[1, i],
                    device_id={"dp": other}, device_id_type=MESH,
                )
                copy.start()
                copy.wait()
                total = total + sums_got[i]
            sum_ref[...] = total

    def tick(j):
        return jnp.minimum(j, 2 * n - 1)

    def gu_out(j):
        k = jnp.clip(j - 4, 0, 2 * n - 1)
        return (1 - k // n, 0, k % n)

    def d_out(j):
        k = jnp.maximum(j - 5, 0) // 2
        k = jnp.where(k < n_dd + skip, jnp.minimum(k, n_dd - 1), jnp.minimum(k - skip, 2 * n_dd - 1))
        return (1 - k // n_dd, 0, k % n_dd)

    anyw = pl.BlockSpec(memory_space=pl.ANY)
    wcol = pl.BlockSpec((None, d, NB), lambda j: (1, 0, jnp.minimum(j, n - 1)))
    wrow = pl.BlockSpec((None, NB, d), lambda j: (1 - tick(j) // n, tick(j) % n, 0))
    out_gu = pl.BlockSpec((None, d // 8, NB), gu_out)
    return pl.pallas_call(
        body,
        grid=(last + 1,),
        in_specs=[anyw] * 6 + [wcol, wcol, wrow],
        out_specs=[out_gu, out_gu, pl.BlockSpec((None, ff // 8, NB), d_out), whole((8, 128))],
        out_shape=[
            jax.ShapeDtypeStruct((2, d // 8, ff), BF),
            jax.ShapeDtypeStruct((2, d // 8, ff), BF),
            jax.ShapeDtypeStruct((2, ff // 8, d), BF),
            jax.ShapeDtypeStruct((8, 128), F32),
        ],
        scratch_shapes=[
            pltpu.VMEM((t_, d), BF),
            pltpu.VMEM((t_, d), BF),
            pltpu.VMEM((t_, d), F32),
            pltpu.VMEM((d, 2 * NB), BF),
            pltpu.VMEM((d, t_), BF),
            pltpu.VMEM((2, t_, NB), F32),
            pltpu.VMEM((4 * DD, t_), BF),
            pltpu.VMEM((t_, 2 * NB), BF),
            pltpu.VMEM((1, NB), F32),
            pltpu.VMEM((3, 8, 128), F32),
            pltpu.VMEM((3, 8, 128), F32),
            pltpu.SemaphoreType.DMA((2, 3)),
            pltpu.SemaphoreType.DMA,
            pltpu.SemaphoreType.DMA,
            pltpu.SemaphoreType.DMA,
            pltpu.SemaphoreType.DMA((2,)),
            pltpu.SemaphoreType.DMA,
        ]
        + exchange_scratch(GU, SLOTS[True])
        + exchange_scratch(DD, SLOTS[False]),
        compiler_params=pltpu.CompilerParams(
            vmem_limit_bytes=VM, dimension_semantics=("arbitrary",), collective_id=1, has_side_effects=True
        ),
        cost_estimate=cost(20 * t_ * d * ff, 0),
        name="backward",
    )(at, dy, h, gate, up, ht, wg, wu, wd)


def swap(bit):
    return [(i, i ^ bit) for i in range(8)]


def send(t, bit):
    return lax.ppermute(t, "dp", swap(bit))


def place(out, pieces, where, shape):
    rows, n = pieces[0].shape
    count = len(pieces)

    def body(*refs):
        pieces, (o_ref, held, sems) = refs[:count], refs[-3:]
        me = lax.axis_index("dp")
        x, y, c = me // 4, me // 2 % 2, me % 2
        loads = [pltpu.make_async_copy(p, held.at[i], sems.at[0, i]) for i, p in enumerate(pieces)]
        stores = []
        for load in loads:
            load.start()
        for i, (load, (layer, fx, fy, fc)) in enumerate(zip(loads, where)):
            block = (abs(fx - x) * 2 + abs(fy - y)) * 2 + abs(fc - c)
            at = pl.ds(pl.multiple_of(block * rows, rows), rows)
            load.wait()
            stores.append(pltpu.make_async_copy(held.at[i], o_ref.at[layer, at], sems.at[1, i]))
            stores[-1].start()
        for store in stores:
            store.wait()

    args = (*pieces, *(() if out is None else (out,)))
    return pl.pallas_call(
        body,
        in_specs=[pl.BlockSpec(memory_space=pl.ANY)] * len(args),
        out_specs=pl.BlockSpec(memory_space=pl.ANY),
        out_shape=jax.ShapeDtypeStruct(shape, BF),
        scratch_shapes=[pltpu.VMEM((count, rows, n), BF), pltpu.SemaphoreType.DMA((2, count))],
        input_output_aliases={} if out is None else {count: 0},
        cost_estimate=cost(2_000_000_000 * count, 4 * count * rows * n),
        name="place",
    )(*args)


def gathered(owns, shapes, others):
    first = [(own, send(own, 4), send(own, 2), send(own, 1)) for own in owns]
    outs, corners, before = [None] * len(shapes), [], None
    for i, (own, from_x, from_y, from_c) in enumerate(first):
        n, l = divmod(i, 2)
        if i:
            from_x, from_y, outs[before] = lax.optimization_barrier((from_x, from_y, outs[before]))
        corners.append(send(*((from_y, 4) if l else (from_x, 2))))
        pieces = own, from_c, from_x, from_y, send(from_x, 1), send(from_y, 1)
        where = (l, 0, 0, 0), (l, 0, 0, 1), (l, 1, 0, 0), (l, 0, 1, 0), (l, 1, 0, 1), (l, 0, 1, 1)
        outs[n] = place(outs[n], pieces, where, shapes[n])
        before = n
    corners[0], outs[before], *others = lax.optimization_barrier((corners[0], outs[before], *others))
    where = (0, 1, 1, 0), (1, 1, 1, 0), (0, 1, 1, 1), (1, 1, 1, 1)
    for n in range(len(outs)):
        pair = corners[2 * n : 2 * n + 2]
        if n:
            *pair, outs[n - 1] = lax.optimization_barrier((*pair, outs[n - 1]))
        pieces = *pair, *(send(t, 1) for t in pair)
        outs[n] = place(outs[n], pieces, where, shapes[n])
    return outs, others


def moments_of(m, v, g):
    return 0.9 * m + 0.1 * g, 0.95 * v + 0.05 * g * g


def weight_of(w, m, v):
    return (w - 0.02 * (m * lax.rsqrt(v + 1e-8) + 0.1 * w)).astype(BF)


def solution(mesh):
    def step(x, dy, wg, wu, wd, *moments):
        me = lax.axis_index("dp")
        x, dy = x[0], dy[0]

        gate, up, ht, at, h = forward(x, wg, wu, wd)
        *grads, total = backward(at, dy, h, gate, up, ht, wg, wu, wd)
        count = sum(w.size for w in (wg, wu, wd))
        factor = jnp.minimum(1.0, 0.5 * lax.rsqrt(total[0, 0] / count + 1e-30))
        weights, m, v = (wg, wu, wd), moments[:3], moments[3:]
        owns, now = [], factor
        for n, w in enumerate(weights):
            rows = m[n].shape[1]
            for l in range(w.shape[0]):
                own = lax.dynamic_slice(w, (l, me * rows, 0), (1, rows, w.shape[2]))[0]
                own = weight_of(own.astype(F32), *moments_of(m[n][l], v[n][l], grads[n][l].astype(F32) * now))
                own, now = lax.optimization_barrier((own, now))
                owns.append(own)
        new = [moments_of(m[n], v[n], grads[n].astype(F32) * now) for n in range(3)]
        outs, others = gathered(owns, [w.shape for w in weights], [t for pair in zip(*new) for t in pair])
        return (*outs, *others)

    P = jax.sharding.PartitionSpec
    rows = P(None, "dp", None)
    return jax.shard_map(
        step,
        mesh=mesh,
        in_specs=(P(("rep", "dp")),) * 2 + (P(),) * 3 + (rows,) * 6,
        out_specs=(P("rep"),) * 3 + (P("rep", "dp", None),) * 6,
        check_vma=False,
    )
```

time: 522 us -> 497 us (0.952)
  Pallas kernels: 327 us -> 306 us
    pallas_call x3 -> x2, Pallas kernels: 297 us -> 276 us  [the longest x1 200 us: backward(): pl.pallas_call(body, grid=(last + 1,), in_specs=[anyw] * 6 + [wcol, wcol,...]
  transfers between devices with their start and end apart: 42 -> 42, of which waited for: 20 -> 20; matrix products, arithmetic and copies ran while one was open for 6% -> 7% of each run, Pallas kernels for 5% -> 5%
where the time goes in v1:
time: 497 us
  Pallas kernels  306 us (62%)
  waiting for transfers between devices  123 us (25%)
  other arithmetic  38.4 us (8%)
  starting transfers between devices  22.5 us (5%)
  local copies, waits for them, and re-layouts  5.26 us (1%)
    pallas_call x1, Pallas kernels, backward(): pl.pallas_call(body, grid=(last + 1,), in_specs=[anyw] * 6 + [wcol, wcol,...  200 us
    ppermute x42, waiting for transfers between devices, send(): return lax.ppermute(t, 'dp', swap(bit))  123 us
    pallas_call x1, Pallas kernels, forward(): pl.pallas_call(body, grid=(2 * n1 + n2,), in_specs=[anyw, wcol, wcol, any...  75.9 us
    pallas_call x9, Pallas kernels, place(): pl.pallas_call(body, in_specs=[pl.BlockSpec(memory_space=pl.ANY)] * len(a...  29.8 us
    ppermute x42, starting transfers between devices, send(): return lax.ppermute(t, 'dp', swap(bit))  22.5 us
    convert_element_type x6, other arithmetic, weight_of(): return (w - 0.02 * (m * lax.rsqrt(v + 1e-08) + 0.1 * w)).astype(BF)  22.1 us
    add x2, other arithmetic, moments_of(): return (0.9 * m + 0.1 * g, 0.95 * v + 0.05 * g * g)  16.2 us
  transfers between devices with their start and end apart: 42, of which 20 were waited for; matrix products, arithmetic and copies ran while one was open for 7% of the time, Pallas kernels for 5%

profile of v1, /device:TPU:0, one launch (start us, length us, event | category | flops | bytes accessed | tf_op | source)
XLA Modules:
  0.0 496.8 jit_solution(6354089640078585001)
XLA Ops:
  0.6 75.9 %forward.1 = (f32[2,2048,2816]{2,1,0:T(8,128)}, f32[2,2048,2816]{2,1,0:T(8,128)}, bf16[2,2816,2048]{2,1,0:T(8,128)(2,1)}, bf16[2,1024,2048]{2,1,0:T(8,128)(2,1)}, bf16[2048,1024]{1,0:T(8,128)(2,1)}) custom-call(bf16[2048,1024]{1,0:T(8,128)(2,1)} %bitcast.87, bf16[2,1024,2816]{2,1,0:T(8,128)(2,1)} %wg_ref.3, bf16[2,1024,2816]{2,1,0:T(8,128)(2,1)} %wu_ref.3, ...), custom_call_target="tpu_custom_call" | custom-call | flops 59055800320 | tf_op jit(solution)/shard_map/forward/pallas_call | solution.py:123
  76.6 200.1 %backward.1 = (bf16[2,128,2816]{2,1,0:T(8,128)(2,1)}, bf16[2,128,2816]{2,1,0:T(8,128)(2,1)}, bf16[2,352,1024]{2,1,0:T(8,128)(2,1)}, f32[8,128]{1,0:T(8,128)}) custom-call(bf16[2,1024,2048]{2,1,0:T(8,128)(2,1)} %get-tuple-element.59.at_hbm, bf16[2048,1024]{1,0:T(8,128)(2,1)} %bitcast.88, bf16[2048,1024]{1,0:T(8,128)(2,1)} %get-tuple-element.60.h_hbm, ...), custom_call_target="tpu_custom_call" | custom-call | flops 118111600640 | tf_op jit(solution)/shard_map/backward/pallas_call | solution.py:417
  278.6 3.2 fusion.5.refs_0_
  282.5 1.3 collective-permute-start.7
  283.8 14.6 %collective-permute-done.6.refs_2_ = bf16[128,2816]{1,0:T(8,128)(2,1)S(1)} collective-permute-done((bf16[128,2816]{1,0:T(8,128)(2,1)S(1)}, bf16[128,2816]{1,0:T(8,128)(2,1)S(1)}, u32[]{:S(2)}, u32[]{:S(2)}) %collective-permute-start.6) | collective-permute-done | bytes 720928 | tf_op jit(solution)/shard_map/ppermute | solution.py:462
  298.9 3.4 fusion.8.refs_0_
  302.4 1.3 collective-permute-start.3
  306.1 3.6 place.9.refs_6_
  309.7 11.3 %collective-permute-done.3.refs_2_ = bf16[128,2816]{1,0:T(8,128)(2,1)} collective-permute-done((bf16[128,2816]{1,0:T(8,128)(2,1)}, bf16[128,2816]{1,0:T(8,128)(2,1)}, u32[]{:S(2)}, u32[]{:S(2)}) %collective-permute-start.3) | collective-permute-done | bytes 720928 | tf_op jit(solution)/shard_map/ppermute | solution.py:462
  322.6 3.9 fusion.11.refs_0_
  328.5 3.6 place.10.refs_4_
  332.1 12.7 %collective-permute-done.refs_2_ = bf16[128,2816]{1,0:T(8,128)(2,1)} collective-permute-done((bf16[128,2816]{1,0:T(8,128)(2,1)}, bf16[128,2816]{1,0:T(8,128)(2,1)}, u32[]{:S(2)}, u32[]{:S(2)}) %collective-permute-start) | collective-permute-done | bytes 720928 | tf_op jit(solution)/shard_map/ppermute | solution.py:462
  345.7 3.9 fusion.14.refs_0_
  351.6 3.6 place.11.refs_6_
  355.2 12.7 %collective-permute-done.13.refs_2_ = bf16[128,2816]{1,0:T(8,128)(2,1)} collective-permute-done((bf16[128,2816]{1,0:T(8,128)(2,1)}, bf16[128,2816]{1,0:T(8,128)(2,1)}, u32[]{:S(2)}, u32[]{:S(2)}) %collective-permute-start.13) | collective-permute-done | bytes 720928 | tf_op jit(solution)/shard_map/ppermute | solution.py:462
  369.5 3.9 fusion.17.refs_0_
  375.4 3.6 place.12.refs_4_
  379.0 12.7 %collective-permute-done.24.refs_2_ = bf16[352,1024]{1,0:T(8,128)(2,1)} collective-permute-done((bf16[352,1024]{1,0:T(8,128)(2,1)}, bf16[352,1024]{1,0:T(8,128)(2,1)}, u32[]{:S(2)}, u32[]{:S(2)}) %collective-permute-start.24) | collective-permute-done | bytes 720928 | tf_op jit(solution)/shard_map/ppermute | solution.py:462
  392.7 3.9 fusion.20.refs_0_
  398.6 1.3 collective-permute-start.33
  400.0 3.6 place.13.refs_6_
  403.6 12.3 %collective-permute-done.21.refs_2_ = bf16[352,1024]{1,0:T(8,128)(2,1)} collective-permute-done((bf16[352,1024]{1,0:T(8,128)(2,1)}, bf16[352,1024]{1,0:T(8,128)(2,1)}, u32[]{:S(2)}, u32[]{:S(2)}) %collective-permute-start.21) | collective-permute-done | bytes 720928 | tf_op jit(solution)/shard_map/ppermute | solution.py:462
  416.5 9.5 %fusion = (f32[2,128,2816]{2,1,0:T(8,128)}, f32[2,128,2816]{2,1,0:T(8,128)}, f32[2,128,2816]{2,1,0:T(8,128)}, f32[2,128,2816]{2,1,0:T(8,128)}) fusion(f32[2,128,2816]{2,1,0:T(8,128)S(1)} %copy-done, bf16[2,128,2816]{2,1,0:T(8,128)(2,1)} %get-tuple-element.65, f32[]{:T(128)} %bitcast.8, f32[2,128,2816]{2,1,0:T(8,128)} %param.16, ...), kind=kLoop, calls=%fused_computation.3 | loop fusion | flops 12976128 | bytes 25952260 | tf_op jit(solution)/shard_map/add | solution.py:523
  426.0 6.7 %fusion.2 = (f32[2,352,1024]{2,1,0:T(8,128)}, f32[2,352,1024]{2,1,0:T(8,128)}) fusion(f32[2,352,1024]{2,1,0:T(8,128)} %param.21, bf16[2,352,1024]{2,1,0:T(8,128)(2,1)S(1)} %copy-done.1, f32[]{:T(128)} %bitcast.8, f32[2,352,1024]{2,1,0:T(8,128)} %param.18), kind=kLoop, calls=%fused_computation.5 | loop fusion | flops 6488064 | bytes 12976132 | tf_op jit(solution)/shard_map/add | solution.py:523
  434.0 3.6 place.14.refs_4_
  437.6 13.2 %collective-permute-done.19.refs_0_ = bf16[128,2816]{1,0:T(8,128)(2,1)S(1)} collective-permute-done((bf16[128,2816]{1,0:T(8,128)(2,1)S(1)}, bf16[128,2816]{1,0:T(8,128)(2,1)S(1)}, u32[]{:S(2)}, u32[]{:S(2)}) %collective-permute-start.19) | collective-permute-done | bytes 720928 | tf_op jit(solution)/shard_map/ppermute | solution.py:462
  453.7 2.7 place.15
  456.5 13.1 %collective-permute-done.12.refs_0_ = bf16[128,2816]{1,0:T(8,128)(2,1)S(1)} collective-permute-done((bf16[128,2816]{1,0:T(8,128)(2,1)}, bf16[128,2816]{1,0:T(8,128)(2,1)S(1)}, u32[]{:S(2)}, u32[]{:S(2)}) %collective-permute-start.12) | collective-permute-done | bytes 720928 | tf_op jit(solution)/shard_map/ppermute | solution.py:462
  474.0 2.8 place.16
  476.7 12.6 %collective-permute-done.36.refs_0_ = bf16[352,1024]{1,0:T(8,128)(2,1)S(1)} collective-permute-done((bf16[352,1024]{1,0:T(8,128)(2,1)}, bf16[352,1024]{1,0:T(8,128)(2,1)S(1)}, u32[]{:S(2)}, u32[]{:S(2)}) %collective-permute-start.36) | collective-permute-done | bytes 720928 | tf_op jit(solution)/shard_map/ppermute | solution.py:462
  490.3 1.7 collective-permute-done.40.refs_2_
  493.9 2.7 place.17
  (108 shorter events, 30.0 us)
Async XLA Ops:
  281.8 16.7 %collective-permute-start.6 = (bf16[128,2816]{1,0:T(8,128)(2,1)S(1)}, bf16[128,2816]{1,0:T(8,128)(2,1)S(1)}, u32[]{:S(2)}, u32[]{:S(2)}) collective-permute-start(bf16[128,2816]{1,0:T(8,128)(2,1)S(1)} %fusion.5.refs_0_), channel_id=1, source_target_pairs={{0,4},{1,5},{2,6},{3,7},{4,0},{5,1},{6,2},{7,3}} | collective-permute-start | bytes 2162696 | tf_op jit(solution)/shard_map/ppermute | solution.py:462
  282.5 16.4 %collective-permute-start.7 = (bf16[128,2816]{1,0:T(8,128)(2,1)S(1)}, bf16[128,2816]{1,0:T(8,128)(2,1)S(1)}, u32[]{:S(2)}, u32[]{:S(2)}) collective-permute-start(bf16[128,2816]{1,0:T(8,128)(2,1)S(1)} %fusion.5.refs_0_), channel_id=1, source_target_pairs={{0,2},{1,3},{2,0},{3,1},{4,6},{5,7},{6,4},{7,5}} | collective-permute-start | bytes 2162696 | tf_op jit(solution)/shard_map/ppermute | solution.py:462
  283.8 20.6 %collective-permute-start.5 = (bf16[128,2816]{1,0:T(8,128)(2,1)S(1)}, bf16[128,2816]{1,0:T(8,128)(2,1)S(1)}, u32[]{:S(2)}, u32[]{:S(2)}) collective-permute-start(bf16[128,2816]{1,0:T(8,128)(2,1)S(1)} %fusion.5.refs_0_), channel_id=1, source_target_pairs={{0,1},{1,0},{2,3},{3,2},{4,5},{5,4},{6,7},{7,6}} | collective-permute-start | bytes 2162696 | tf_op jit(solution)/shard_map/ppermute | solution.py:462
  298.9 7.3 %collective-permute-start.9 = (bf16[128,2816]{1,0:T(8,128)(2,1)S(1)}, bf16[128,2816]{1,0:T(8,128)(2,1)}, u32[]{:S(2)}, u32[]{:S(2)}) collective-permute-start(bf16[128,2816]{1,0:T(8,128)(2,1)S(1)} %collective-permute-done.7.refs_3_), channel_id=1, source_target_pairs={{0,1},{1,0},{2,3},{3,2},{4,5},{5,4},{6,7},{7,6}} | collective-permute-start | bytes 2162696 | tf_op jit(solution)/shard_map/ppermute | solution.py:462
  302.4 18.6 %collective-permute-start.3 = (bf16[128,2816]{1,0:T(8,128)(2,1)}, bf16[128,2816]{1,0:T(8,128)(2,1)}, u32[]{:S(2)}, u32[]{:S(2)}) collective-permute-start(bf16[128,2816]{1,0:T(8,128)(2,1)} %fusion.8.refs_0_), channel_id=1, source_target_pairs={{0,4},{1,5},{2,6},{3,7},{4,0},{5,1},{6,2},{7,3}} | collective-permute-start | bytes 2162696 | tf_op jit(solution)/shard_map/ppermute | solution.py:462
  303.7 18.3 %collective-permute-start.4 = (bf16[128,2816]{1,0:T(8,128)(2,1)}, bf16[128,2816]{1,0:T(8,128)(2,1)}, u32[]{:S(2)}, u32[]{:S(2)}) collective-permute-start(bf16[128,2816]{1,0:T(8,128)(2,1)} %fusion.8.refs_0_), channel_id=1, source_target_pairs={{0,2},{1,3},{2,0},{3,1},{4,6},{5,7},{6,4},{7,5}} | collective-permute-start | bytes 2162696 | tf_op jit(solution)/shard_map/ppermute | solution.py:462
  304.4 24.0 %collective-permute-start.2 = (bf16[128,2816]{1,0:T(8,128)(2,1)}, bf16[128,2816]{1,0:T(8,128)(2,1)}, u32[]{:S(2)}, u32[]{:S(2)}) collective-permute-start(bf16[128,2816]{1,0:T(8,128)(2,1)} %fusion.8.refs_0_), channel_id=1, source_target_pairs={{0,1},{1,0},{2,3},{3,2},{4,5},{5,4},{6,7},{7,6}} | collective-permute-start | bytes 2162696 | tf_op jit(solution)/shard_map/ppermute | solution.py:462
  326.4 18.4 %collective-permute-start = (bf16[128,2816]{1,0:T(8,128)(2,1)}, bf16[128,2816]{1,0:T(8,128)(2,1)}, u32[]{:S(2)}, u32[]{:S(2)}) collective-permute-start(bf16[128,2816]{1,0:T(8,128)(2,1)} %fusion.11.refs_0_), channel_id=1, source_target_pairs={{0,4},{1,5},{2,6},{3,7},{4,0},{5,1},{6,2},{7,3}} | collective-permute-start | bytes 2162696 | tf_op jit(solution)/shard_map/ppermute | solution.py:462
  327.1 18.1 %collective-permute-start.1 = (bf16[128,2816]{1,0:T(8,128)(2,1)}, bf16[128,2816]{1,0:T(8,128)(2,1)}, u32[]{:S(2)}, u32[]{:S(2)}) collective-permute-start(bf16[128,2816]{1,0:T(8,128)(2,1)} %fusion.11.refs_0_), channel_id=1, source_target_pairs={{0,2},{1,3},{2,0},{3,1},{4,6},{5,7},{6,4},{7,5}} | collective-permute-start | bytes 2162696 | tf_op jit(solution)/shard_map/ppermute | solution.py:462
  328.5 23.2 %collective-permute-start.15 = (bf16[128,2816]{1,0:T(8,128)(2,1)}, bf16[128,2816]{1,0:T(8,128)(2,1)}, u32[]{:S(2)}, u32[]{:S(2)}) collective-permute-start(bf16[128,2816]{1,0:T(8,128)(2,1)} %fusion.11.refs_0_), channel_id=1, source_target_pairs={{0,1},{1,0},{2,3},{3,2},{4,5},{5,4},{6,7},{7,6}} | collective-permute-start | bytes 2162696 | tf_op jit(solution)/shard_map/ppermute | solution.py:462
  349.6 18.4 %collective-permute-start.13 = (bf16[128,2816]{1,0:T(8,128)(2,1)}, bf16[128,2816]{1,0:T(8,128)(2,1)}, u32[]{:S(2)}, u32[]{:S(2)}) collective-permute-start(bf16[128,2816]{1,0:T(8,128)(2,1)} %fusion.14.refs_0_), channel_id=1, source_target_pairs={{0,4},{1,5},{2,6},{3,7},{4,0},{5,1},{6,2},{7,3}} | collective-permute-start | bytes 2162696 | tf_op jit(solution)/shard_map/ppermute | solution.py:462
  350.9 18.1 %collective-permute-start.14 = (bf16[128,2816]{1,0:T(8,128)(2,1)}, bf16[128,2816]{1,0:T(8,128)(2,1)}, u32[]{:S(2)}, u32[]{:S(2)}) collective-permute-start(bf16[128,2816]{1,0:T(8,128)(2,1)} %fusion.14.refs_0_), channel_id=1, source_target_pairs={{0,2},{1,3},{2,0},{3,1},{4,6},{5,7},{6,4},{7,5}} | collective-permute-start | bytes 2162696 | tf_op jit(solution)/shard_map/ppermute | solution.py:462
  351.6 23.8 %collective-permute-start.26 = (bf16[128,2816]{1,0:T(8,128)(2,1)}, bf16[128,2816]{1,0:T(8,128)(2,1)}, u32[]{:S(2)}, u32[]{:S(2)}) collective-permute-start(bf16[128,2816]{1,0:T(8,128)(2,1)} %fusion.14.refs_0_), channel_id=1, source_target_pairs={{0,1},{1,0},{2,3},{3,2},{4,5},{5,4},{6,7},{7,6}} | collective-permute-start | bytes 2162696 | tf_op jit(solution)/shard_map/ppermute | solution.py:462
  369.0 6.4 %collective-permute-start.27 = (bf16[128,2816]{1,0:T(8,128)(2,1)}, bf16[128,2816]{1,0:T(8,128)(2,1)}, u32[]{:S(2)}, u32[]{:S(2)}) collective-permute-start(bf16[128,2816]{1,0:T(8,128)(2,1)} %collective-permute-done.13.refs_2_), channel_id=1, source_target_pairs={{0,1},{1,0},{2,3},{3,2},{4,5},{5,4},{6,7},{7,6}} | collective-permute-start | bytes 2162696 | tf_op jit(solution)/shard_map/ppermute | solution.py:462
  369.0 6.4 %collective-permute-start.28 = (bf16[128,2816]{1,0:T(8,128)(2,1)}, bf16[128,2816]{1,0:T(8,128)(2,1)}, u32[]{:S(2)}, u32[]{:S(2)}) collective-permute-start(bf16[128,2816]{1,0:T(8,128)(2,1)} %collective-permute-done.14.refs_3_), channel_id=1, source_target_pairs={{0,1},{1,0},{2,3},{3,2},{4,5},{5,4},{6,7},{7,6}} | collective-permute-start | bytes 2162696 | tf_op jit(solution)/shard_map/ppermute | solution.py:462
  373.4 18.4 %collective-permute-start.24 = (bf16[352,1024]{1,0:T(8,128)(2,1)}, bf16[352,1024]{1,0:T(8,128)(2,1)}, u32[]{:S(2)}, u32[]{:S(2)}) collective-permute-start(bf16[352,1024]{1,0:T(8,128)(2,1)} %fusion.17.refs_0_), channel_id=1, source_target_pairs={{0,4},{1,5},{2,6},{3,7},{4,0},{5,1},{6,2},{7,3}} | collective-permute-start | bytes 2162696 | tf_op jit(solution)/shard_map/ppermute | solution.py:462
  374.1 18.1 %collective-permute-start.25 = (bf16[352,1024]{1,0:T(8,128)(2,1)}, bf16[352,1024]{1,0:T(8,128)(2,1)}, u32[]{:S(2)}, u32[]{:S(2)}) collective-permute-start(bf16[352,1024]{1,0:T(8,128)(2,1)} %fusion.17.refs_0_), channel_id=1, source_target_pairs={{0,2},{1,3},{2,0},{3,1},{4,6},{5,7},{6,4},{7,5}} | collective-permute-start | bytes 2162696 | tf_op jit(solution)/shard_map/ppermute | solution.py:462
  375.4 23.2 %collective-permute-start.23 = (bf16[352,1024]{1,0:T(8,128)(2,1)}, bf16[352,1024]{1,0:T(8,128)(2,1)}, u32[]{:S(2)}, u32[]{:S(2)}) collective-permute-start(bf16[352,1024]{1,0:T(8,128)(2,1)} %fusion.17.refs_0_), channel_id=1, source_target_pairs={{0,1},{1,0},{2,3},{3,2},{4,5},{5,4},{6,7},{7,6}} | collective-permute-start | bytes 2162696 | tf_op jit(solution)/shard_map/ppermute | solution.py:462
  392.2 6.5 %collective-permute-start.29 = (bf16[352,1024]{1,0:T(8,128)(2,1)}, bf16[352,1024]{1,0:T(8,128)(2,1)}, u32[]{:S(2)}, u32[]{:S(2)}) collective-permute-start(bf16[352,1024]{1,0:T(8,128)(2,1)} %collective-permute-done.24.refs_2_), channel_id=1, source_target_pairs={{0,1},{1,0},{2,3},{3,2},{4,5},{5,4},{6,7},{7,6}} | collective-permute-start | bytes 2162696 | tf_op jit(solution)/shard_map/ppermute | solution.py:462
  392.2 7.8 %collective-permute-start.30 = (bf16[352,1024]{1,0:T(8,128)(2,1)}, bf16[352,1024]{1,0:T(8,128)(2,1)}, u32[]{:S(2)}, u32[]{:S(2)}) collective-permute-start(bf16[352,1024]{1,0:T(8,128)(2,1)} %collective-permute-done.25.refs_3_), channel_id=1, source_target_pairs={{0,1},{1,0},{2,3},{3,2},{4,5},{5,4},{6,7},{7,6}} | collective-permute-start | bytes 2162696 | tf_op jit(solution)/shard_map/ppermute | solution.py:462
  396.6 19.3 %collective-permute-start.21 = (bf16[352,1024]{1,0:T(8,128)(2,1)}, bf16[352,1024]{1,0:T(8,128)(2,1)}, u32[]{:S(2)}, u32[]{:S(2)}) collective-permute-start(bf16[352,1024]{1,0:T(8,128)(2,1)} %fusion.20.refs_0_), channel_id=1, source_target_pairs={{0,4},{1,5},{2,6},{3,7},{4,0},{5,1},{6,2},{7,3}} | collective-permute-start | bytes 2162696 | tf_op jit(solution)/shard_map/ppermute | solution.py:462
  397.9 18.1 %collective-permute-start.22 = (bf16[352,1024]{1,0:T(8,128)(2,1)}, bf16[352,1024]{1,0:T(8,128)(2,1)}, u32[]{:S(2)}, u32[]{:S(2)}) collective-permute-start(bf16[352,1024]{1,0:T(8,128)(2,1)} %fusion.20.refs_0_), channel_id=1, source_target_pairs={{0,2},{1,3},{2,0},{3,1},{4,6},{5,7},{6,4},{7,5}} | collective-permute-start | bytes 2162696 | tf_op jit(solution)/shard_map/ppermute | solution.py:462
  398.6 35.4 %collective-permute-start.20 = (bf16[352,1024]{1,0:T(8,128)(2,1)}, bf16[352,1024]{1,0:T(8,128)(2,1)}, u32[]{:S(2)}, u32[]{:S(2)}) collective-permute-start(bf16[352,1024]{1,0:T(8,128)(2,1)} %fusion.20.refs_0_), channel_id=1, source_target_pairs={{0,1},{1,0},{2,3},{3,2},{4,5},{5,4},{6,7},{7,6}} | collective-permute-start | bytes 2162696 | tf_op jit(solution)/shard_map/ppermute | solution.py:462
  398.6 35.4 %collective-permute-start.33 = (bf16[128,2816]{1,0:T(8,128)(2,1)}, bf16[128,2816]{1,0:T(8,128)(2,1)}, u32[]{:S(2)}, u32[]{:S(2)}) collective-permute-start(bf16[128,2816]{1,0:T(8,128)(2,1)} %collective-permute-done.4.refs_3_), channel_id=1, source_target_pairs={{0,4},{1,5},{2,6},{3,7},{4,0},{5,1},{6,2},{7,3}} | collective-permute-start | bytes 2162696 | tf_op jit(solution)/shard_map/ppermute | solution.py:462
  416.0 18.0 %collective-permute-start.31 = (bf16[352,1024]{1,0:T(8,128)(2,1)}, bf16[352,1024]{1,0:T(8,128)(2,1)}, u32[]{:S(2)}, u32[]{:S(2)}) collective-permute-start(bf16[352,1024]{1,0:T(8,128)(2,1)} %collective-permute-done.21.refs_2_), channel_id=1, source_target_pairs={{0,1},{1,0},{2,3},{3,2},{4,5},{5,4},{6,7},{7,6}} | collective-permute-start | bytes 2162696 | tf_op jit(solution)/shard_map/ppermute | solution.py:462
  416.0 18.0 %collective-permute-start.32 = (bf16[352,1024]{1,0:T(8,128)(2,1)}, bf16[352,1024]{1,0:T(8,128)(2,1)}, u32[]{:S(2)}, u32[]{:S(2)}) collective-permute-start(bf16[352,1024]{1,0:T(8,128)(2,1)} %collective-permute-done.22.refs_3_), channel_id=1, source_target_pairs={{0,1},{1,0},{2,3},{3,2},{4,5},{5,4},{6,7},{7,6}} | collective-permute-start | bytes 2162696 | tf_op jit(solution)/shard_map/ppermute | solution.py:462
  432.8 18.0 %collective-permute-start.19 = (bf16[128,2816]{1,0:T(8,128)(2,1)S(1)}, bf16[128,2816]{1,0:T(8,128)(2,1)S(1)}, u32[]{:S(2)}, u32[]{:S(2)}) collective-permute-start(bf16[128,2816]{1,0:T(8,128)(2,1)S(1)} %copy-done.5), channel_id=1, source_target_pairs={{0,2},{1,3},{2,0},{3,1},{4,6},{5,7},{6,4},{7,5}} | collective-permute-start | bytes 2162696 | tf_op jit(solution)/shard_map/ppermute | solution.py:462
  434.0 18.8 %collective-permute-start.35 = (bf16[128,2816]{1,0:T(8,128)(2,1)}, bf16[128,2816]{1,0:T(8,128)(2,1)S(1)}, u32[]{:S(2)}, u32[]{:S(2)}) collective-permute-start(bf16[128,2816]{1,0:T(8,128)(2,1)} %collective-permute-done.33.refs_1_), channel_id=1, source_target_pairs={{0,1},{1,0},{2,3},{3,2},{4,5},{5,4},{6,7},{7,6}} | collective-permute-start | bytes 2162696 | tf_op jit(solution)/shard_map/ppermute | solution.py:462
  450.8 18.8 %collective-permute-start.12 = (bf16[128,2816]{1,0:T(8,128)(2,1)}, bf16[128,2816]{1,0:T(8,128)(2,1)S(1)}, u32[]{:S(2)}, u32[]{:S(2)}) collective-permute-start(bf16[128,2816]{1,0:T(8,128)(2,1)} %collective-permute-done.refs_2_), channel_id=1, source_target_pairs={{0,2},{1,3},{2,0},{3,1},{4,6},{5,7},{6,4},{7,5}} | collective-permute-start | bytes 2162696 | tf_op jit(solution)/shard_map/ppermute | solution.py:462
  452.1 18.5 %collective-permute-start.18 = (bf16[128,2816]{1,0:T(8,128)(2,1)}, bf16[128,2816]{1,0:T(8,128)(2,1)S(1)}, u32[]{:S(2)}, u32[]{:S(2)}) collective-permute-start(bf16[128,2816]{1,0:T(8,128)(2,1)} %collective-permute-done.14.refs_3_), channel_id=1, source_target_pairs={{0,4},{1,5},{2,6},{3,7},{4,0},{5,1},{6,2},{7,3}} | collective-permute-start | bytes 2162696 | tf_op jit(solution)/shard_map/ppermute | solution.py:462
  471.1 18.3 %collective-permute-start.36 = (bf16[352,1024]{1,0:T(8,128)(2,1)}, bf16[352,1024]{1,0:T(8,128)(2,1)S(1)}, u32[]{:S(2)}, u32[]{:S(2)}) collective-permute-start(bf16[352,1024]{1,0:T(8,128)(2,1)} %collective-permute-done.24.refs_2_), channel_id=1, source_target_pairs={{0,2},{1,3},{2,0},{3,1},{4,6},{5,7},{6,4},{7,5}} | collective-permute-start | bytes 2162696 | tf_op jit(solution)/shard_map/ppermute | solution.py:462
  471.8 18.0 %collective-permute-start.37 = (bf16[352,1024]{1,0:T(8,128)(2,1)}, bf16[352,1024]{1,0:T(8,128)(2,1)S(1)}, u32[]{:S(2)}, u32[]{:S(2)}) collective-permute-start(bf16[352,1024]{1,0:T(8,128)(2,1)} %collective-permute-done.22.refs_3_), channel_id=1, source_target_pairs={{0,4},{1,5},{2,6},{3,7},{4,0},{5,1},{6,2},{7,3}} | collective-permute-start | bytes 2162696 | tf_op jit(solution)/shard_map/ppermute | solution.py:462
  (28 other events, 165.9 us)

commit v2 on v1

--- a/solution.py
+++ b/solution.py
@@ -166,14 +166,15 @@
         self.src, self.rc, self.sx, self.sy, self.rx, self.ry, self.s2, self.r2 = src, rc, sx, sy, rx, ry, s2, r2
         self.sent, self.got, self.squares, self.put = sent, got, squares, put
         me = lax.axis_index("dp")
+        self.me, self.others = me, [lax.rem(me + i, 8) for i in range(1, 8)]
         self.x, self.y, self.c = me // 4, me // 2 % 2, me % 2
         self.over_c, self.over_y, self.over_x = me + 1 - 2 * self.c, me + 2 - 4 * self.y, me + 4 - 8 * self.x
 
     def barrier(self):
         b = pltpu.get_barrier_semaphore()
-        for other in (self.over_c, self.over_y, self.over_x):
+        for other in self.others:
             pl.semaphore_signal(b, inc=1, device_id={"dp": other}, device_id_type=MESH)
-        pl.semaphore_wait(b, 3)
+        pl.semaphore_wait(b, len(self.others))
 
     def copy(self, n, slot, src, dst, other):
         return pltpu.make_async_remote_copy(
@@ -252,10 +253,11 @@
     ff = wg.shape[2]
     n, n_dd = ff // NB, d // NB
     last = 2 * n + 3
+    count = wg.size + wu.size + wd.size
     skip = (n + 1) // 2 - n_dd
 
     def body(
-        at_hbm, dy_hbm, h_hbm, g_hbm, u_hbm, ht_hbm, wg_ref, wu_ref, wd_ref, rg_ref, ru_ref, rd_ref, sum_ref,
+        at_hbm, dy_hbm, h_hbm, g_hbm, u_hbm, ht_hbm, wg_ref, wu_ref, wd_ref, rg_ref, ru_ref, rd_ref, factor_ref,
         dh, hs, acc, w, at, gu, hbuf, dgu, sq, sums, sums_got, sums_sem, at_sem, dh_sem, h_sem, gu_sem, ht_sem, *refs,
     ):
         src, src_d = refs[0], refs[10]
@@ -386,17 +388,25 @@
 
         @pl.when(t == last)
         def _():
-            total = jnp.broadcast_to(jnp.sum(sq[...], 1, keepdims=True), (8, 128))
-            for i, other in enumerate((ex.over_c, ex.over_y, ex.over_x)):
-                sums[i] = total
-                copy = pltpu.make_async_remote_copy(
-                    src_ref=sums.at[i], dst_ref=sums_got.at[i], send_sem=sums_sem.at[0, i], recv_sem=sums_sem.at[1, i],
+            own = jnp.broadcast_to(jnp.sum(sq[...], 1, keepdims=True), (8, 128))
+            sums[...] = own
+            sums_got[ex.me] = own
+            copies = [
+                pltpu.make_async_remote_copy(
+                    src_ref=sums, dst_ref=sums_got.at[ex.me], send_sem=sums_sem.at[0, i], recv_sem=sums_sem.at[1, i],
                     device_id={"dp": other}, device_id_type=MESH,
                 )
+                for i, other in enumerate(ex.others)
+            ]
+            for copy in copies:
                 copy.start()
+            for copy in copies:
                 copy.wait()
+            total = sums_got[0]
+            for i in range(1, 8):
                 total = total + sums_got[i]
-            sum_ref[...] = total
+            factor = jnp.minimum(1.0, 0.5 * lax.rsqrt(total / count + 1e-30))
+            factor_ref[...] = factor[:1, :1]
 
     def tick(j):
         return jnp.minimum(j, 2 * n - 1)
@@ -418,12 +428,12 @@
         body,
         grid=(last + 1,),
         in_specs=[anyw] * 6 + [wcol, wcol, wrow],
-        out_specs=[out_gu, out_gu, pl.BlockSpec((None, ff // 8, NB), d_out), whole((8, 128))],
+        out_specs=[out_gu, out_gu, pl.BlockSpec((None, ff // 8, NB), d_out), whole((1, 1))],
         out_shape=[
             jax.ShapeDtypeStruct((2, d // 8, ff), BF),
             jax.ShapeDtypeStruct((2, d // 8, ff), BF),
             jax.ShapeDtypeStruct((2, ff // 8, d), BF),
-            jax.ShapeDtypeStruct((8, 128), F32),
+            jax.ShapeDtypeStruct((1, 1), F32),
         ],
         scratch_shapes=[
             pltpu.VMEM((t_, d), BF),
@@ -435,9 +445,9 @@
             pltpu.VMEM((4 * DD, t_), BF),
             pltpu.VMEM((t_, 2 * NB), BF),
             pltpu.VMEM((1, NB), F32),
-            pltpu.VMEM((3, 8, 128), F32),
-            pltpu.VMEM((3, 8, 128), F32),
-            pltpu.SemaphoreType.DMA((2, 3)),
+            pltpu.VMEM((8, 128), F32),
+            pltpu.VMEM((8, 8, 128), F32),
+            pltpu.SemaphoreType.DMA((2, 7)),
             pltpu.SemaphoreType.DMA,
             pltpu.SemaphoreType.DMA,
             pltpu.SemaphoreType.DMA,
@@ -491,6 +501,7 @@
         out_shape=jax.ShapeDtypeStruct(shape, BF),
         scratch_shapes=[pltpu.VMEM((count, rows, n), BF), pltpu.SemaphoreType.DMA((2, count))],
         input_output_aliases={} if out is None else {count: 0},
+        compiler_params=pltpu.CompilerParams(vmem_limit_bytes=VM),
         cost_estimate=cost(2_000_000_000 * count, 4 * count * rows * n),
         name="place",
     )(*args)
@@ -533,9 +544,8 @@
         x, dy = x[0], dy[0]
 
         gate, up, ht, at, h = forward(x, wg, wu, wd)
-        *grads, total = backward(at, dy, h, gate, up, ht, wg, wu, wd)
-        count = sum(w.size for w in (wg, wu, wd))
-        factor = jnp.minimum(1.0, 0.5 * lax.rsqrt(total[0, 0] / count + 1e-30))
+        *grads, factor = backward(at, dy, h, gate, up, ht, wg, wu, wd)
+        factor = factor[0, 0]
         weights, m, v = (wg, wu, wd), moments[:3], moments[3:]
         owns, now = [], factor
         for n, w in enumerate(weights):

time: 497 us -> 498 us (level)
  transfers between devices with their start and end apart: 42 -> 42, of which waited for: 20 -> 22; matrix products, arithmetic and copies ran while one was open for 7% -> 8% of each run, Pallas kernels for 5% -> 5%
where the time goes in v2:
time: 498 us; the launch traced here: 497 us
  Pallas kernels  302 us (61%)
  waiting for transfers between devices  127 us (26%)
  other arithmetic  42.7 us (9%)
  starting transfers between devices  23.2 us (5%)
    pallas_call x1, Pallas kernels, backward(): pl.pallas_call(body, grid=(last + 1,), in_specs=[anyw] * 6 + [wcol, wcol,...  196 us
    ppermute x42, waiting for transfers between devices, send(): return lax.ppermute(t, 'dp', swap(bit))  127 us
    pallas_call x1, Pallas kernels, forward(): pl.pallas_call(body, grid=(2 * n1 + n2,), in_specs=[anyw, wcol, wcol, any...  75.9 us
    pallas_call x9, Pallas kernels, place(): pl.pallas_call(body, in_specs=[pl.BlockSpec(memory_space=pl.ANY)] * len(a...  29.8 us
    convert_element_type x6, other arithmetic, weight_of(): return (w - 0.02 * (m * lax.rsqrt(v + 1e-08) + 0.1 * w)).astype(BF)  25.6 us
    ppermute x42, starting transfers between devices, send(): return lax.ppermute(t, 'dp', swap(bit))  23.2 us
    add x2, other arithmetic, moments_of(): return (0.9 * m + 0.1 * g, 0.95 * v + 0.05 * g * g)  17.1 us
  transfers between devices with their start and end apart: 42, of which 22 were waited for; matrix products, arithmetic and copies ran while one was open for 8% of the time, Pallas kernels for 5%

profile of v2, /device:TPU:0, one launch (start us, length us, event | category | flops | bytes accessed | tf_op | source)
XLA Modules:
  0.0 497.0 jit_solution(13024062821368301713)
XLA Ops:
  0.6 75.9 %forward.1 = (f32[2,2048,2816]{2,1,0:T(8,128)}, f32[2,2048,2816]{2,1,0:T(8,128)}, bf16[2,2816,2048]{2,1,0:T(8,128)(2,1)}, bf16[2,1024,2048]{2,1,0:T(8,128)(2,1)}, bf16[2048,1024]{1,0:T(8,128)(2,1)}) custom-call(bf16[2048,1024]{1,0:T(8,128)(2,1)} %bitcast.87, bf16[2,1024,2816]{2,1,0:T(8,128)(2,1)} %wg_ref.3, bf16[2,1024,2816]{2,1,0:T(8,128)(2,1)} %wu_ref.3, ...), custom_call_target="tpu_custom_call" | custom-call | flops 59055800320 | tf_op jit(solution)/shard_map/forward/pallas_call | solution.py:123
  76.5 196.2 %backward.1 = (bf16[2,128,2816]{2,1,0:T(8,128)(2,1)}, bf16[2,128,2816]{2,1,0:T(8,128)(2,1)}, bf16[2,352,1024]{2,1,0:T(8,128)(2,1)}, f32[1,1]{1,0:T(1,128)}) custom-call(bf16[2,1024,2048]{2,1,0:T(8,128)(2,1)} %get-tuple-element.59.at_hbm, bf16[2048,1024]{1,0:T(8,128)(2,1)} %bitcast.88, bf16[2048,1024]{1,0:T(8,128)(2,1)} %get-tuple-element.60.h_hbm, ...), custom_call_target="tpu_custom_call" | custom-call | flops 118111600640 | tf_op jit(solution)/shard_map/backward/pallas_call | solution.py:427
  272.8 4.1 fusion.5.refs_0_
  277.5 1.5 collective-permute-start.7
  279.0 16.2 %collective-permute-done.6.refs_2_ = bf16[128,2816]{1,0:T(8,128)(2,1)} collective-permute-done((bf16[128,2816]{1,0:T(8,128)(2,1)S(1)}, bf16[128,2816]{1,0:T(8,128)(2,1)}, u32[]{:S(2)}, u32[]{:S(2)}) %collective-permute-start.6) | collective-permute-done | bytes 720928 | tf_op jit(solution)/shard_map/ppermute | solution.py:472
  295.6 3.8 fusion.8.refs_0_
  302.4 3.6 place.9.refs_6_
  306.0 12.0 %collective-permute-done.3.refs_2_ = bf16[128,2816]{1,0:T(8,128)(2,1)} collective-permute-done((bf16[128,2816]{1,0:T(8,128)(2,1)}, bf16[128,2816]{1,0:T(8,128)(2,1)}, u32[]{:S(2)}, u32[]{:S(2)}) %collective-permute-start.3) | collective-permute-done | bytes 720928 | tf_op jit(solution)/shard_map/ppermute | solution.py:472
  319.7 4.4 fusion.11.refs_0_
  326.2 3.6 place.10.refs_4_
  329.8 12.6 %collective-permute-done.refs_2_ = bf16[128,2816]{1,0:T(8,128)(2,1)} collective-permute-done((bf16[128,2816]{1,0:T(8,128)(2,1)}, bf16[128,2816]{1,0:T(8,128)(2,1)}, u32[]{:S(2)}, u32[]{:S(2)}) %collective-permute-start) | collective-permute-done | bytes 720928 | tf_op jit(solution)/shard_map/ppermute | solution.py:472
  343.3 4.4 fusion.14.refs_0_
  349.8 3.6 place.11.refs_6_
  353.4 12.7 %collective-permute-done.13.refs_2_ = bf16[128,2816]{1,0:T(8,128)(2,1)} collective-permute-done((bf16[128,2816]{1,0:T(8,128)(2,1)}, bf16[128,2816]{1,0:T(8,128)(2,1)}, u32[]{:S(2)}, u32[]{:S(2)}) %collective-permute-start.13) | collective-permute-done | bytes 720928 | tf_op jit(solution)/shard_map/ppermute | solution.py:472
  367.7 4.4 fusion.17.refs_0_
  372.8 1.5 collective-permute-start.25
  374.3 3.6 place.12.refs_4_
  377.9 12.6 %collective-permute-done.24.refs_2_ = bf16[352,1024]{1,0:T(8,128)(2,1)} collective-permute-done((bf16[352,1024]{1,0:T(8,128)(2,1)}, bf16[352,1024]{1,0:T(8,128)(2,1)}, u32[]{:S(2)}, u32[]{:S(2)}) %collective-permute-start.24) | collective-permute-done | bytes 720928 | tf_op jit(solution)/shard_map/ppermute | solution.py:472
  391.4 4.4 fusion.20.refs_0_
  397.9 1.5 collective-permute-start.33
  399.4 3.6 place.13.refs_6_
  403.0 12.2 %collective-permute-done.21.refs_2_ = bf16[352,1024]{1,0:T(8,128)(2,1)} collective-permute-done((bf16[352,1024]{1,0:T(8,128)(2,1)}, bf16[352,1024]{1,0:T(8,128)(2,1)}, u32[]{:S(2)}, u32[]{:S(2)}) %collective-permute-start.21) | collective-permute-done | bytes 720928 | tf_op jit(solution)/shard_map/ppermute | solution.py:472
  415.8 11.1 %fusion = (f32[2,128,2816]{2,1,0:T(8,128)}, f32[2,128,2816]{2,1,0:T(8,128)}, f32[2,128,2816]{2,1,0:T(8,128)}, f32[2,128,2816]{2,1,0:T(8,128)}) fusion(f32[2,128,2816]{2,1,0:T(8,128)} %param.19, bf16[2,128,2816]{2,1,0:T(8,128)(2,1)} %get-tuple-element.65, f32[]{:T(128)} %bitcast.8, f32[2,128,2816]{2,1,0:T(8,128)} %param.16, ...), kind=kLoop, calls=%fused_computation.3 | loop fusion | flops 12976128 | bytes 25952260 | tf_op jit(solution)/shard_map/add | solution.py:534
  427.0 6.0 %fusion.2 = (f32[2,352,1024]{2,1,0:T(8,128)}, f32[2,352,1024]{2,1,0:T(8,128)}) fusion(f32[2,352,1024]{2,1,0:T(8,128)S(1)} %copy-done.1, bf16[2,352,1024]{2,1,0:T(8,128)(2,1)S(1)} %copy-done.2, f32[]{:T(128)} %bitcast.8, f32[2,352,1024]{2,1,0:T(8,128)} %param.18), kind=kLoop, calls=%fused_computation.5 | loop fusion | flops 6488064 | bytes 12976132 | tf_op jit(solution)/shard_map/add | solution.py:534
  434.3 3.6 place.14.refs_4_
  437.9 13.4 %collective-permute-done.19.refs_0_ = bf16[128,2816]{1,0:T(8,128)(2,1)} collective-permute-done((bf16[128,2816]{1,0:T(8,128)(2,1)}, bf16[128,2816]{1,0:T(8,128)(2,1)}, u32[]{:S(2)}, u32[]{:S(2)}) %collective-permute-start.19) | collective-permute-done | bytes 720928 | tf_op jit(solution)/shard_map/ppermute | solution.py:472
  453.9 2.7 place.15
  456.6 13.6 %collective-permute-done.12.refs_0_ = bf16[128,2816]{1,0:T(8,128)(2,1)} collective-permute-done((bf16[128,2816]{1,0:T(8,128)(2,1)}, bf16[128,2816]{1,0:T(8,128)(2,1)}, u32[]{:S(2)}, u32[]{:S(2)}) %collective-permute-start.12) | collective-permute-done | bytes 720928 | tf_op jit(solution)/shard_map/ppermute | solution.py:472
  474.8 2.7 place.16
  477.6 12.6 %collective-permute-done.36.refs_0_ = bf16[352,1024]{1,0:T(8,128)(2,1)} collective-permute-done((bf16[352,1024]{1,0:T(8,128)(2,1)}, bf16[352,1024]{1,0:T(8,128)(2,1)}, u32[]{:S(2)}, u32[]{:S(2)}) %collective-permute-start.36) | collective-permute-done | bytes 720928 | tf_op jit(solution)/shard_map/ppermute | solution.py:472
  491.1 2.0 collective-permute-done.40.refs_2_
  494.1 2.7 place.17
  (85 shorter events, 27.1 us)
Async XLA Ops:
  276.8 18.3 %collective-permute-start.6 = (bf16[128,2816]{1,0:T(8,128)(2,1)S(1)}, bf16[128,2816]{1,0:T(8,128)(2,1)}, u32[]{:S(2)}, u32[]{:S(2)}) collective-permute-start(bf16[128,2816]{1,0:T(8,128)(2,1)S(1)} %fusion.5.refs_0_), channel_id=1, source_target_pairs={{0,4},{1,5},{2,6},{3,7},{4,0},{5,1},{6,2},{7,3}} | collective-permute-start | bytes 2162696 | tf_op jit(solution)/shard_map/ppermute | solution.py:472
  277.5 17.9 %collective-permute-start.7 = (bf16[128,2816]{1,0:T(8,128)(2,1)S(1)}, bf16[128,2816]{1,0:T(8,128)(2,1)S(1)}, u32[]{:S(2)}, u32[]{:S(2)}) collective-permute-start(bf16[128,2816]{1,0:T(8,128)(2,1)S(1)} %fusion.5.refs_0_), channel_id=1, source_target_pairs={{0,2},{1,3},{2,0},{3,1},{4,6},{5,7},{6,4},{7,5}} | collective-permute-start | bytes 2162696 | tf_op jit(solution)/shard_map/ppermute | solution.py:472
  279.0 22.6 %collective-permute-start.5 = (bf16[128,2816]{1,0:T(8,128)(2,1)S(1)}, bf16[128,2816]{1,0:T(8,128)(2,1)S(1)}, u32[]{:S(2)}, u32[]{:S(2)}) collective-permute-start(bf16[128,2816]{1,0:T(8,128)(2,1)S(1)} %fusion.5.refs_0_), channel_id=1, source_target_pairs={{0,1},{1,0},{2,3},{3,2},{4,5},{5,4},{6,7},{7,6}} | collective-permute-start | bytes 2162696 | tf_op jit(solution)/shard_map/ppermute | solution.py:472
  295.1 7.3 %collective-permute-start.8 = (bf16[128,2816]{1,0:T(8,128)(2,1)}, bf16[128,2816]{1,0:T(8,128)(2,1)}, u32[]{:S(2)}, u32[]{:S(2)}) collective-permute-start(bf16[128,2816]{1,0:T(8,128)(2,1)} %collective-permute-done.6.refs_2_), channel_id=1, source_target_pairs={{0,1},{1,0},{2,3},{3,2},{4,5},{5,4},{6,7},{7,6}} | collective-permute-start | bytes 2162696 | tf_op jit(solution)/shard_map/ppermute | solution.py:472
  295.4 7.1 %collective-permute-start.9 = (bf16[128,2816]{1,0:T(8,128)(2,1)S(1)}, bf16[128,2816]{1,0:T(8,128)(2,1)}, u32[]{:S(2)}, u32[]{:S(2)}) collective-permute-start(bf16[128,2816]{1,0:T(8,128)(2,1)S(1)} %collective-permute-done.7.refs_3_), channel_id=1, source_target_pairs={{0,1},{1,0},{2,3},{3,2},{4,5},{5,4},{6,7},{7,6}} | collective-permute-start | bytes 2162696 | tf_op jit(solution)/shard_map/ppermute | solution.py:472
  299.5 18.6 %collective-permute-start.3 = (bf16[128,2816]{1,0:T(8,128)(2,1)}, bf16[128,2816]{1,0:T(8,128)(2,1)}, u32[]{:S(2)}, u32[]{:S(2)}) collective-permute-start(bf16[128,2816]{1,0:T(8,128)(2,1)} %fusion.8.refs_0_), channel_id=1, source_target_pairs={{0,4},{1,5},{2,6},{3,7},{4,0},{5,1},{6,2},{7,3}} | collective-permute-start | bytes 2162696 | tf_op jit(solution)/shard_map/ppermute | solution.py:472
  300.6 18.6 %collective-permute-start.4 = (bf16[128,2816]{1,0:T(8,128)(2,1)}, bf16[128,2816]{1,0:T(8,128)(2,1)}, u32[]{:S(2)}, u32[]{:S(2)}) collective-permute-start(bf16[128,2816]{1,0:T(8,128)(2,1)} %fusion.8.refs_0_), channel_id=1, source_target_pairs={{0,2},{1,3},{2,0},{3,1},{4,6},{5,7},{6,4},{7,5}} | collective-permute-start | bytes 2162696 | tf_op jit(solution)/shard_map/ppermute | solution.py:472
  302.4 23.8 %collective-permute-start.2 = (bf16[128,2816]{1,0:T(8,128)(2,1)}, bf16[128,2816]{1,0:T(8,128)(2,1)}, u32[]{:S(2)}, u32[]{:S(2)}) collective-permute-start(bf16[128,2816]{1,0:T(8,128)(2,1)} %fusion.8.refs_0_), channel_id=1, source_target_pairs={{0,1},{1,0},{2,3},{3,2},{4,5},{5,4},{6,7},{7,6}} | collective-permute-start | bytes 2162696 | tf_op jit(solution)/shard_map/ppermute | solution.py:472
  324.1 18.4 %collective-permute-start = (bf16[128,2816]{1,0:T(8,128)(2,1)}, bf16[128,2816]{1,0:T(8,128)(2,1)}, u32[]{:S(2)}, u32[]{:S(2)}) collective-permute-start(bf16[128,2816]{1,0:T(8,128)(2,1)} %fusion.11.refs_0_), channel_id=1, source_target_pairs={{0,4},{1,5},{2,6},{3,7},{4,0},{5,1},{6,2},{7,3}} | collective-permute-start | bytes 2162696 | tf_op jit(solution)/shard_map/ppermute | solution.py:472
  324.7 18.1 %collective-permute-start.1 = (bf16[128,2816]{1,0:T(8,128)(2,1)}, bf16[128,2816]{1,0:T(8,128)(2,1)}, u32[]{:S(2)}, u32[]{:S(2)}) collective-permute-start(bf16[128,2816]{1,0:T(8,128)(2,1)} %fusion.11.refs_0_), channel_id=1, source_target_pairs={{0,2},{1,3},{2,0},{3,1},{4,6},{5,7},{6,4},{7,5}} | collective-permute-start | bytes 2162696 | tf_op jit(solution)/shard_map/ppermute | solution.py:472
  326.2 23.6 %collective-permute-start.15 = (bf16[128,2816]{1,0:T(8,128)(2,1)}, bf16[128,2816]{1,0:T(8,128)(2,1)}, u32[]{:S(2)}, u32[]{:S(2)}) collective-permute-start(bf16[128,2816]{1,0:T(8,128)(2,1)} %fusion.11.refs_0_), channel_id=1, source_target_pairs={{0,1},{1,0},{2,3},{3,2},{4,5},{5,4},{6,7},{7,6}} | collective-permute-start | bytes 2162696 | tf_op jit(solution)/shard_map/ppermute | solution.py:472
  347.8 18.4 %collective-permute-start.13 = (bf16[128,2816]{1,0:T(8,128)(2,1)}, bf16[128,2816]{1,0:T(8,128)(2,1)}, u32[]{:S(2)}, u32[]{:S(2)}) collective-permute-start(bf16[128,2816]{1,0:T(8,128)(2,1)} %fusion.14.refs_0_), channel_id=1, source_target_pairs={{0,4},{1,5},{2,6},{3,7},{4,0},{5,1},{6,2},{7,3}} | collective-permute-start | bytes 2162696 | tf_op jit(solution)/shard_map/ppermute | solution.py:472
  349.1 18.1 %collective-permute-start.14 = (bf16[128,2816]{1,0:T(8,128)(2,1)}, bf16[128,2816]{1,0:T(8,128)(2,1)}, u32[]{:S(2)}, u32[]{:S(2)}) collective-permute-start(bf16[128,2816]{1,0:T(8,128)(2,1)} %fusion.14.refs_0_), channel_id=1, source_target_pairs={{0,2},{1,3},{2,0},{3,1},{4,6},{5,7},{6,4},{7,5}} | collective-permute-start | bytes 2162696 | tf_op jit(solution)/shard_map/ppermute | solution.py:472
  349.8 24.5 %collective-permute-start.26 = (bf16[128,2816]{1,0:T(8,128)(2,1)}, bf16[128,2816]{1,0:T(8,128)(2,1)}, u32[]{:S(2)}, u32[]{:S(2)}) collective-permute-start(bf16[128,2816]{1,0:T(8,128)(2,1)} %fusion.14.refs_0_), channel_id=1, source_target_pairs={{0,1},{1,0},{2,3},{3,2},{4,5},{5,4},{6,7},{7,6}} | collective-permute-start | bytes 2162696 | tf_op jit(solution)/shard_map/ppermute | solution.py:472
  367.2 7.1 %collective-permute-start.27 = (bf16[128,2816]{1,0:T(8,128)(2,1)}, bf16[128,2816]{1,0:T(8,128)(2,1)}, u32[]{:S(2)}, u32[]{:S(2)}) collective-permute-start(bf16[128,2816]{1,0:T(8,128)(2,1)} %collective-permute-done.13.refs_2_), channel_id=1, source_target_pairs={{0,1},{1,0},{2,3},{3,2},{4,5},{5,4},{6,7},{7,6}} | collective-permute-start | bytes 2162696 | tf_op jit(solution)/shard_map/ppermute | solution.py:472
  367.2 7.1 %collective-permute-start.28 = (bf16[128,2816]{1,0:T(8,128)(2,1)}, bf16[128,2816]{1,0:T(8,128)(2,1)}, u32[]{:S(2)}, u32[]{:S(2)}) collective-permute-start(bf16[128,2816]{1,0:T(8,128)(2,1)} %collective-permute-done.14.refs_3_), channel_id=1, source_target_pairs={{0,1},{1,0},{2,3},{3,2},{4,5},{5,4},{6,7},{7,6}} | collective-permute-start | bytes 2162696 | tf_op jit(solution)/shard_map/ppermute | solution.py:472
  372.2 18.4 %collective-permute-start.24 = (bf16[352,1024]{1,0:T(8,128)(2,1)}, bf16[352,1024]{1,0:T(8,128)(2,1)}, u32[]{:S(2)}, u32[]{:S(2)}) collective-permute-start(bf16[352,1024]{1,0:T(8,128)(2,1)} %fusion.17.refs_0_), channel_id=1, source_target_pairs={{0,4},{1,5},{2,6},{3,7},{4,0},{5,1},{6,2},{7,3}} | collective-permute-start | bytes 2162696 | tf_op jit(solution)/shard_map/ppermute | solution.py:472
  372.8 18.1 %collective-permute-start.25 = (bf16[352,1024]{1,0:T(8,128)(2,1)}, bf16[352,1024]{1,0:T(8,128)(2,1)}, u32[]{:S(2)}, u32[]{:S(2)}) collective-permute-start(bf16[352,1024]{1,0:T(8,128)(2,1)} %fusion.17.refs_0_), channel_id=1, source_target_pairs={{0,2},{1,3},{2,0},{3,1},{4,6},{5,7},{6,4},{7,5}} | collective-permute-start | bytes 2162696 | tf_op jit(solution)/shard_map/ppermute | solution.py:472
  374.3 23.6 %collective-permute-start.23 = (bf16[352,1024]{1,0:T(8,128)(2,1)}, bf16[352,1024]{1,0:T(8,128)(2,1)}, u32[]{:S(2)}, u32[]{:S(2)}) collective-permute-start(bf16[352,1024]{1,0:T(8,128)(2,1)} %fusion.17.refs_0_), channel_id=1, source_target_pairs={{0,1},{1,0},{2,3},{3,2},{4,5},{5,4},{6,7},{7,6}} | collective-permute-start | bytes 2162696 | tf_op jit(solution)/shard_map/ppermute | solution.py:472
  390.9 8.5 %collective-permute-start.30 = (bf16[352,1024]{1,0:T(8,128)(2,1)}, bf16[352,1024]{1,0:T(8,128)(2,1)}, u32[]{:S(2)}, u32[]{:S(2)}) collective-permute-start(bf16[352,1024]{1,0:T(8,128)(2,1)} %collective-permute-done.25.refs_3_), channel_id=1, source_target_pairs={{0,1},{1,0},{2,3},{3,2},{4,5},{5,4},{6,7},{7,6}} | collective-permute-start | bytes 2162696 | tf_op jit(solution)/shard_map/ppermute | solution.py:472
  395.8 19.3 %collective-permute-start.21 = (bf16[352,1024]{1,0:T(8,128)(2,1)}, bf16[352,1024]{1,0:T(8,128)(2,1)}, u32[]{:S(2)}, u32[]{:S(2)}) collective-permute-start(bf16[352,1024]{1,0:T(8,128)(2,1)} %fusion.20.refs_0_), channel_id=1, source_target_pairs={{0,4},{1,5},{2,6},{3,7},{4,0},{5,1},{6,2},{7,3}} | collective-permute-start | bytes 2162696 | tf_op jit(solution)/shard_map/ppermute | solution.py:472
  397.2 18.1 %collective-permute-start.22 = (bf16[352,1024]{1,0:T(8,128)(2,1)}, bf16[352,1024]{1,0:T(8,128)(2,1)}, u32[]{:S(2)}, u32[]{:S(2)}) collective-permute-start(bf16[352,1024]{1,0:T(8,128)(2,1)} %fusion.20.refs_0_), channel_id=1, source_target_pairs={{0,2},{1,3},{2,0},{3,1},{4,6},{5,7},{6,4},{7,5}} | collective-permute-start | bytes 2162696 | tf_op jit(solution)/shard_map/ppermute | solution.py:472
  397.9 36.4 %collective-permute-start.20 = (bf16[352,1024]{1,0:T(8,128)(2,1)}, bf16[352,1024]{1,0:T(8,128)(2,1)}, u32[]{:S(2)}, u32[]{:S(2)}) collective-permute-start(bf16[352,1024]{1,0:T(8,128)(2,1)} %fusion.20.refs_0_), channel_id=1, source_target_pairs={{0,1},{1,0},{2,3},{3,2},{4,5},{5,4},{6,7},{7,6}} | collective-permute-start | bytes 2162696 | tf_op jit(solution)/shard_map/ppermute | solution.py:472
  397.9 36.4 %collective-permute-start.33 = (bf16[128,2816]{1,0:T(8,128)(2,1)}, bf16[128,2816]{1,0:T(8,128)(2,1)}, u32[]{:S(2)}, u32[]{:S(2)}) collective-permute-start(bf16[128,2816]{1,0:T(8,128)(2,1)} %collective-permute-done.4.refs_3_), channel_id=1, source_target_pairs={{0,4},{1,5},{2,6},{3,7},{4,0},{5,1},{6,2},{7,3}} | collective-permute-start | bytes 2162696 | tf_op jit(solution)/shard_map/ppermute | solution.py:472
  415.3 19.0 %collective-permute-start.31 = (bf16[352,1024]{1,0:T(8,128)(2,1)}, bf16[352,1024]{1,0:T(8,128)(2,1)}, u32[]{:S(2)}, u32[]{:S(2)}) collective-permute-start(bf16[352,1024]{1,0:T(8,128)(2,1)} %collective-permute-done.21.refs_2_), channel_id=1, source_target_pairs={{0,1},{1,0},{2,3},{3,2},{4,5},{5,4},{6,7},{7,6}} | collective-permute-start | bytes 2162696 | tf_op jit(solution)/shard_map/ppermute | solution.py:472
  415.3 19.0 %collective-permute-start.32 = (bf16[352,1024]{1,0:T(8,128)(2,1)}, bf16[352,1024]{1,0:T(8,128)(2,1)}, u32[]{:S(2)}, u32[]{:S(2)}) collective-permute-start(bf16[352,1024]{1,0:T(8,128)(2,1)} %collective-permute-done.22.refs_3_), channel_id=1, source_target_pairs={{0,1},{1,0},{2,3},{3,2},{4,5},{5,4},{6,7},{7,6}} | collective-permute-start | bytes 2162696 | tf_op jit(solution)/shard_map/ppermute | solution.py:472
  433.0 18.4 %collective-permute-start.19 = (bf16[128,2816]{1,0:T(8,128)(2,1)}, bf16[128,2816]{1,0:T(8,128)(2,1)}, u32[]{:S(2)}, u32[]{:S(2)}) collective-permute-start(bf16[128,2816]{1,0:T(8,128)(2,1)} %collective-permute-done.6.refs_2_), channel_id=1, source_target_pairs={{0,2},{1,3},{2,0},{3,1},{4,6},{5,7},{6,4},{7,5}} | collective-permute-start | bytes 2162696 | tf_op jit(solution)/shard_map/ppermute | solution.py:472
  434.3 19.1 %collective-permute-start.35 = (bf16[128,2816]{1,0:T(8,128)(2,1)}, bf16[128,2816]{1,0:T(8,128)(2,1)}, u32[]{:S(2)}, u32[]{:S(2)}) collective-permute-start(bf16[128,2816]{1,0:T(8,128)(2,1)} %collective-permute-done.33.refs_1_), channel_id=1, source_target_pairs={{0,1},{1,0},{2,3},{3,2},{4,5},{5,4},{6,7},{7,6}} | collective-permute-start | bytes 2162696 | tf_op jit(solution)/shard_map/ppermute | solution.py:472
  451.3 18.9 %collective-permute-start.12 = (bf16[128,2816]{1,0:T(8,128)(2,1)}, bf16[128,2816]{1,0:T(8,128)(2,1)}, u32[]{:S(2)}, u32[]{:S(2)}) collective-permute-start(bf16[128,2816]{1,0:T(8,128)(2,1)} %collective-permute-done.refs_2_), channel_id=1, source_target_pairs={{0,2},{1,3},{2,0},{3,1},{4,6},{5,7},{6,4},{7,5}} | collective-permute-start | bytes 2162696 | tf_op jit(solution)/shard_map/ppermute | solution.py:472
  452.7 18.6 %collective-permute-start.18 = (bf16[128,2816]{1,0:T(8,128)(2,1)}, bf16[128,2816]{1,0:T(8,128)(2,1)}, u32[]{:S(2)}, u32[]{:S(2)}) collective-permute-start(bf16[128,2816]{1,0:T(8,128)(2,1)} %collective-permute-done.14.refs_3_), channel_id=1, source_target_pairs={{0,4},{1,5},{2,6},{3,7},{4,0},{5,1},{6,2},{7,3}} | collective-permute-start | bytes 2162696 | tf_op jit(solution)/shard_map/ppermute | solution.py:472
  471.8 18.4 %collective-permute-start.36 = (bf16[352,1024]{1,0:T(8,128)(2,1)}, bf16[352,1024]{1,0:T(8,128)(2,1)}, u32[]{:S(2)}, u32[]{:S(2)}) collective-permute-start(bf16[352,1024]{1,0:T(8,128)(2,1)} %collective-permute-done.24.refs_2_), channel_id=1, source_target_pairs={{0,2},{1,3},{2,0},{3,1},{4,6},{5,7},{6,4},{7,5}} | collective-permute-start | bytes 2162696 | tf_op jit(solution)/shard_map/ppermute | solution.py:472
  472.5 18.1 %collective-permute-start.37 = (bf16[352,1024]{1,0:T(8,128)(2,1)}, bf16[352,1024]{1,0:T(8,128)(2,1)}, u32[]{:S(2)}, u32[]{:S(2)}) collective-permute-start(bf16[352,1024]{1,0:T(8,128)(2,1)} %collective-permute-done.22.refs_3_), channel_id=1, source_target_pairs={{0,4},{1,5},{2,6},{3,7},{4,0},{5,1},{6,2},{7,3}} | collective-permute-start | bytes 2162696 | tf_op jit(solution)/shard_map/ppermute | solution.py:472
  (17 other events, 158.3 us)

commit v3 on v2

--- a/solution.py
+++ b/solution.py
@@ -525,8 +525,9 @@
         pair = corners[2 * n : 2 * n + 2]
         if n:
             *pair, outs[n - 1] = lax.optimization_barrier((*pair, outs[n - 1]))
-        pieces = *pair, *(send(t, 1) for t in pair)
-        outs[n] = place(outs[n], pieces, where, shapes[n])
+        swapped = [send(t, 1) for t in pair]
+        outs[n] = place(outs[n], pair, where[:2], shapes[n])
+        outs[n] = place(outs[n], swapped, where[2:], shapes[n])
     return outs, others
 
 

time: 498 us -> 497 us (level)
  Pallas kernels: 302 us -> 307 us
  waiting for transfers between devices: 127 us -> 122 us
    ppermute x42, waiting for transfers between devices: 127 us -> 122 us  [send(): return lax.ppermute(t, 'dp', swap(bit))]
    pallas_call x9 -> x12, Pallas kernels: 29.8 us -> 35 us  [place(): pl.pallas_call(body, in_specs=[pl.BlockSpec(memory_space=pl.ANY)] * len(a...]
  transfers between devices with their start and end apart: 42 -> 42, of which waited for: 22 -> 18; matrix products, arithmetic and copies ran while one was open for 8% -> 8% of each run, Pallas kernels for 5% -> 7%
where the time goes in v3:
time: 497 us
  Pallas kernels  307 us (62%)
  waiting for transfers between devices  122 us (25%)
  other arithmetic  42.7 us (9%)
  starting transfers between devices  23.2 us (5%)
    pallas_call x1, Pallas kernels, backward(): pl.pallas_call(body, grid=(last + 1,), in_specs=[anyw] * 6 + [wcol, wcol,...  196 us
    ppermute x42, waiting for transfers between devices, send(): return lax.ppermute(t, 'dp', swap(bit))  122 us
    pallas_call x1, Pallas kernels, forward(): pl.pallas_call(body, grid=(2 * n1 + n2,), in_specs=[anyw, wcol, wcol, any...  75.9 us
    pallas_call x12, Pallas kernels, place(): pl.pallas_call(body, in_specs=[pl.BlockSpec(memory_space=pl.ANY)] * len(a...  35 us
    convert_element_type x6, other arithmetic, weight_of(): return (w - 0.02 * (m * lax.rsqrt(v + 1e-08) + 0.1 * w)).astype(BF)  25.6 us
    ppermute x42, starting transfers between devices, send(): return lax.ppermute(t, 'dp', swap(bit))  23.2 us
    add x2, other arithmetic, moments_of(): return (0.9 * m + 0.1 * g, 0.95 * v + 0.05 * g * g)  17.1 us
  transfers between devices with their start and end apart: 42, of which 18 were waited for; matrix products, arithmetic and copies ran while one was open for 8% of the time, Pallas kernels for 7%

profile of v3, /device:TPU:0, one launch (start us, length us, event | category | flops | bytes accessed | tf_op | source)
XLA Modules:
  0.0 496.5 jit_solution(5272474054267824278)
XLA Ops:
  0.6 75.9 %forward.1 = (f32[2,2048,2816]{2,1,0:T(8,128)}, f32[2,2048,2816]{2,1,0:T(8,128)}, bf16[2,2816,2048]{2,1,0:T(8,128)(2,1)}, bf16[2,1024,2048]{2,1,0:T(8,128)(2,1)}, bf16[2048,1024]{1,0:T(8,128)(2,1)}) custom-call(bf16[2048,1024]{1,0:T(8,128)(2,1)} %bitcast.87, bf16[2,1024,2816]{2,1,0:T(8,128)(2,1)} %wg_ref.3, bf16[2,1024,2816]{2,1,0:T(8,128)(2,1)} %wu_ref.3, ...), custom_call_target="tpu_custom_call" | custom-call | flops 59055800320 | tf_op jit(solution)/shard_map/forward/pallas_call | solution.py:123
  76.5 196.2 %backward.1 = (bf16[2,128,2816]{2,1,0:T(8,128)(2,1)}, bf16[2,128,2816]{2,1,0:T(8,128)(2,1)}, bf16[2,352,1024]{2,1,0:T(8,128)(2,1)}, f32[1,1]{1,0:T(1,128)}) custom-call(bf16[2,1024,2048]{2,1,0:T(8,128)(2,1)} %get-tuple-element.59.at_hbm, bf16[2048,1024]{1,0:T(8,128)(2,1)} %bitcast.88, bf16[2048,1024]{1,0:T(8,128)(2,1)} %get-tuple-element.60.h_hbm, ...), custom_call_target="tpu_custom_call" | custom-call | flops 118111600640 | tf_op jit(solution)/shard_map/backward/pallas_call | solution.py:427
  272.8 4.1 fusion.5.refs_0_
  279.0 16.2 %collective-permute-done.6.refs_2_ = bf16[128,2816]{1,0:T(8,128)(2,1)} collective-permute-done((bf16[128,2816]{1,0:T(8,128)(2,1)S(1)}, bf16[128,2816]{1,0:T(8,128)(2,1)}, u32[]{:S(2)}, u32[]{:S(2)}) %collective-permute-start.6) | collective-permute-done | bytes 720928 | tf_op jit(solution)/shard_map/ppermute | solution.py:472
  295.6 3.8 fusion.8.refs_0_
  302.4 3.6 place.12.refs_6_
  306.0 12.0 %collective-permute-done.3.refs_2_ = bf16[128,2816]{1,0:T(8,128)(2,1)} collective-permute-done((bf16[128,2816]{1,0:T(8,128)(2,1)}, bf16[128,2816]{1,0:T(8,128)(2,1)}, u32[]{:S(2)}, u32[]{:S(2)}) %collective-permute-start.3) | collective-permute-done | bytes 720928 | tf_op jit(solution)/shard_map/ppermute | solution.py:472
  319.7 4.4 fusion.11.refs_0_
  326.2 3.6 place.13.refs_2_
  329.8 12.6 %collective-permute-done.refs_2_ = bf16[128,2816]{1,0:T(8,128)(2,1)} collective-permute-done((bf16[128,2816]{1,0:T(8,128)(2,1)}, bf16[128,2816]{1,0:T(8,128)(2,1)}, u32[]{:S(2)}, u32[]{:S(2)}) %collective-permute-start) | collective-permute-done | bytes 720928 | tf_op jit(solution)/shard_map/ppermute | solution.py:472
  343.3 4.4 fusion.14.refs_0_
  349.8 3.6 place.14.refs_6_
  353.4 12.7 %collective-permute-done.13.refs_2_ = bf16[128,2816]{1,0:T(8,128)(2,1)} collective-permute-done((bf16[128,2816]{1,0:T(8,128)(2,1)}, bf16[128,2816]{1,0:T(8,128)(2,1)}, u32[]{:S(2)}, u32[]{:S(2)}) %collective-permute-start.13) | collective-permute-done | bytes 720928 | tf_op jit(solution)/shard_map/ppermute | solution.py:472
  367.7 4.4 fusion.17.refs_0_
  374.3 3.6 place.15.refs_2_
  377.9 12.6 %collective-permute-done.24.refs_2_ = bf16[352,1024]{1,0:T(8,128)(2,1)} collective-permute-done((bf16[352,1024]{1,0:T(8,128)(2,1)}, bf16[352,1024]{1,0:T(8,128)(2,1)}, u32[]{:S(2)}, u32[]{:S(2)}) %collective-permute-start.24) | collective-permute-done | bytes 720928 | tf_op jit(solution)/shard_map/ppermute | solution.py:472
  391.4 4.4 fusion.20.refs_0_
  397.9 1.5 collective-permute-start.34
  399.4 3.6 place.16.refs_6_
  403.0 12.2 %collective-permute-done.21.refs_2_ = bf16[352,1024]{1,0:T(8,128)(2,1)} collective-permute-done((bf16[352,1024]{1,0:T(8,128)(2,1)}, bf16[352,1024]{1,0:T(8,128)(2,1)}, u32[]{:S(2)}, u32[]{:S(2)}) %collective-permute-start.21) | collective-permute-done | bytes 720928 | tf_op jit(solution)/shard_map/ppermute | solution.py:472
  415.8 11.1 %fusion = (f32[2,128,2816]{2,1,0:T(8,128)}, f32[2,128,2816]{2,1,0:T(8,128)}, f32[2,128,2816]{2,1,0:T(8,128)}, f32[2,128,2816]{2,1,0:T(8,128)}) fusion(f32[2,128,2816]{2,1,0:T(8,128)} %param.19, bf16[2,128,2816]{2,1,0:T(8,128)(2,1)} %get-tuple-element.65, f32[]{:T(128)} %bitcast.8, f32[2,128,2816]{2,1,0:T(8,128)} %param.16, ...), kind=kLoop, calls=%fused_computation.3 | loop fusion | flops 12976128 | bytes 25952260 | tf_op jit(solution)/shard_map/add | solution.py:535
  427.0 6.0 %fusion.2 = (f32[2,352,1024]{2,1,0:T(8,128)}, f32[2,352,1024]{2,1,0:T(8,128)}) fusion(f32[2,352,1024]{2,1,0:T(8,128)S(1)} %copy-done.1, bf16[2,352,1024]{2,1,0:T(8,128)(2,1)S(1)} %copy-done.2, f32[]{:T(128)} %bitcast.8, f32[2,352,1024]{2,1,0:T(8,128)} %param.18), kind=kLoop, calls=%fused_computation.5 | loop fusion | flops 6488064 | bytes 12976132 | tf_op jit(solution)/shard_map/add | solution.py:535
  434.3 3.6 place.17.refs_2_
  437.9 13.4 %collective-permute-done.19.refs_0_ = bf16[128,2816]{1,0:T(8,128)(2,1)} collective-permute-done((bf16[128,2816]{1,0:T(8,128)(2,1)}, bf16[128,2816]{1,0:T(8,128)(2,1)}, u32[]{:S(2)}, u32[]{:S(2)}) %collective-permute-start.19) | collective-permute-done | bytes 720928 | tf_op jit(solution)/shard_map/ppermute | solution.py:472
  453.4 2.2 place.18.refs_2_
  455.7 2.2 place.19
  458.0 12.2 %collective-permute-done.12.refs_0_ = bf16[128,2816]{1,0:T(8,128)(2,1)} collective-permute-done((bf16[128,2816]{1,0:T(8,128)(2,1)}, bf16[128,2816]{1,0:T(8,128)(2,1)}, u32[]{:S(2)}, u32[]{:S(2)}) %collective-permute-start.12) | collective-permute-done | bytes 720928 | tf_op jit(solution)/shard_map/ppermute | solution.py:472
  473.7 2.2 place.20.refs_2_
  476.0 2.2 place.21
  478.2 11.9 %collective-permute-done.36.refs_0_ = bf16[352,1024]{1,0:T(8,128)(2,1)} collective-permute-done((bf16[352,1024]{1,0:T(8,128)(2,1)}, bf16[352,1024]{1,0:T(8,128)(2,1)}, u32[]{:S(2)}, u32[]{:S(2)}) %collective-permute-start.36) | collective-permute-done | bytes 720928 | tf_op jit(solution)/shard_map/ppermute | solution.py:472
  491.1 2.2 place.22.refs_2_
  494.1 2.2 place.23
  (88 shorter events, 28.3 us)
Async XLA Ops:
  276.8 18.3 %collective-permute-start.6 = (bf16[128,2816]{1,0:T(8,128)(2,1)S(1)}, bf16[128,2816]{1,0:T(8,128)(2,1)}, u32[]{:S(2)}, u32[]{:S(2)}) collective-permute-start(bf16[128,2816]{1,0:T(8,128)(2,1)S(1)} %fusion.5.refs_0_), channel_id=1, source_target_pairs={{0,4},{1,5},{2,6},{3,7},{4,0},{5,1},{6,2},{7,3}} | collective-permute-start | bytes 2162696 | tf_op jit(solution)/shard_map/ppermute | solution.py:472
  277.5 17.9 %collective-permute-start.7 = (bf16[128,2816]{1,0:T(8,128)(2,1)S(1)}, bf16[128,2816]{1,0:T(8,128)(2,1)S(1)}, u32[]{:S(2)}, u32[]{:S(2)}) collective-permute-start(bf16[128,2816]{1,0:T(8,128)(2,1)S(1)} %fusion.5.refs_0_), channel_id=1, source_target_pairs={{0,2},{1,3},{2,0},{3,1},{4,6},{5,7},{6,4},{7,5}} | collective-permute-start | bytes 2162696 | tf_op jit(solution)/shard_map/ppermute | solution.py:472
  279.0 22.6 %collective-permute-start.5 = (bf16[128,2816]{1,0:T(8,128)(2,1)S(1)}, bf16[128,2816]{1,0:T(8,128)(2,1)S(1)}, u32[]{:S(2)}, u32[]{:S(2)}) collective-permute-start(bf16[128,2816]{1,0:T(8,128)(2,1)S(1)} %fusion.5.refs_0_), channel_id=1, source_target_pairs={{0,1},{1,0},{2,3},{3,2},{4,5},{5,4},{6,7},{7,6}} | collective-permute-start | bytes 2162696 | tf_op jit(solution)/shard_map/ppermute | solution.py:472
  295.1 7.3 %collective-permute-start.8 = (bf16[128,2816]{1,0:T(8,128)(2,1)}, bf16[128,2816]{1,0:T(8,128)(2,1)}, u32[]{:S(2)}, u32[]{:S(2)}) collective-permute-start(bf16[128,2816]{1,0:T(8,128)(2,1)} %collective-permute-done.6.refs_2_), channel_id=1, source_target_pairs={{0,1},{1,0},{2,3},{3,2},{4,5},{5,4},{6,7},{7,6}} | collective-permute-start | bytes 2162696 | tf_op jit(solution)/shard_map/ppermute | solution.py:472
  295.4 7.1 %collective-permute-start.9 = (bf16[128,2816]{1,0:T(8,128)(2,1)S(1)}, bf16[128,2816]{1,0:T(8,128)(2,1)}, u32[]{:S(2)}, u32[]{:S(2)}) collective-permute-start(bf16[128,2816]{1,0:T(8,128)(2,1)S(1)} %collective-permute-done.7.refs_3_), channel_id=1, source_target_pairs={{0,1},{1,0},{2,3},{3,2},{4,5},{5,4},{6,7},{7,6}} | collective-permute-start | bytes 2162696 | tf_op jit(solution)/shard_map/ppermute | solution.py:472
  299.5 18.6 %collective-permute-start.3 = (bf16[128,2816]{1,0:T(8,128)(2,1)}, bf16[128,2816]{1,0:T(8,128)(2,1)}, u32[]{:S(2)}, u32[]{:S(2)}) collective-permute-start(bf16[128,2816]{1,0:T(8,128)(2,1)} %fusion.8.refs_0_), channel_id=1, source_target_pairs={{0,4},{1,5},{2,6},{3,7},{4,0},{5,1},{6,2},{7,3}} | collective-permute-start | bytes 2162696 | tf_op jit(solution)/shard_map/ppermute | solution.py:472
  300.6 18.6 %collective-permute-start.4 = (bf16[128,2816]{1,0:T(8,128)(2,1)}, bf16[128,2816]{1,0:T(8,128)(2,1)}, u32[]{:S(2)}, u32[]{:S(2)}) collective-permute-start(bf16[128,2816]{1,0:T(8,128)(2,1)} %fusion.8.refs_0_), channel_id=1, source_target_pairs={{0,2},{1,3},{2,0},{3,1},{4,6},{5,7},{6,4},{7,5}} | collective-permute-start | bytes 2162696 | tf_op jit(solution)/shard_map/ppermute | solution.py:472
  302.4 23.8 %collective-permute-start.2 = (bf16[128,2816]{1,0:T(8,128)(2,1)}, bf16[128,2816]{1,0:T(8,128)(2,1)}, u32[]{:S(2)}, u32[]{:S(2)}) collective-permute-start(bf16[128,2816]{1,0:T(8,128)(2,1)} %fusion.8.refs_0_), channel_id=1, source_target_pairs={{0,1},{1,0},{2,3},{3,2},{4,5},{5,4},{6,7},{7,6}} | collective-permute-start | bytes 2162696 | tf_op jit(solution)/shard_map/ppermute | solution.py:472
  324.1 18.4 %collective-permute-start = (bf16[128,2816]{1,0:T(8,128)(2,1)}, bf16[128,2816]{1,0:T(8,128)(2,1)}, u32[]{:S(2)}, u32[]{:S(2)}) collective-permute-start(bf16[128,2816]{1,0:T(8,128)(2,1)} %fusion.11.refs_0_), channel_id=1, source_target_pairs={{0,4},{1,5},{2,6},{3,7},{4,0},{5,1},{6,2},{7,3}} | collective-permute-start | bytes 2162696 | tf_op jit(solution)/shard_map/ppermute | solution.py:472
  324.7 18.1 %collective-permute-start.1 = (bf16[128,2816]{1,0:T(8,128)(2,1)}, bf16[128,2816]{1,0:T(8,128)(2,1)}, u32[]{:S(2)}, u32[]{:S(2)}) collective-permute-start(bf16[128,2816]{1,0:T(8,128)(2,1)} %fusion.11.refs_0_), channel_id=1, source_target_pairs={{0,2},{1,3},{2,0},{3,1},{4,6},{5,7},{6,4},{7,5}} | collective-permute-start | bytes 2162696 | tf_op jit(solution)/shard_map/ppermute | solution.py:472
  326.2 23.6 %collective-permute-start.15 = (bf16[128,2816]{1,0:T(8,128)(2,1)}, bf16[128,2816]{1,0:T(8,128)(2,1)}, u32[]{:S(2)}, u32[]{:S(2)}) collective-permute-start(bf16[128,2816]{1,0:T(8,128)(2,1)} %fusion.11.refs_0_), channel_id=1, source_target_pairs={{0,1},{1,0},{2,3},{3,2},{4,5},{5,4},{6,7},{7,6}} | collective-permute-start | bytes 2162696 | tf_op jit(solution)/shard_map/ppermute | solution.py:472
  347.8 18.4 %collective-permute-start.13 = (bf16[128,2816]{1,0:T(8,128)(2,1)}, bf16[128,2816]{1,0:T(8,128)(2,1)}, u32[]{:S(2)}, u32[]{:S(2)}) collective-permute-start(bf16[128,2816]{1,0:T(8,128)(2,1)} %fusion.14.refs_0_), channel_id=1, source_target_pairs={{0,4},{1,5},{2,6},{3,7},{4,0},{5,1},{6,2},{7,3}} | collective-permute-start | bytes 2162696 | tf_op jit(solution)/shard_map/ppermute | solution.py:472
  349.1 18.1 %collective-permute-start.14 = (bf16[128,2816]{1,0:T(8,128)(2,1)}, bf16[128,2816]{1,0:T(8,128)(2,1)}, u32[]{:S(2)}, u32[]{:S(2)}) collective-permute-start(bf16[128,2816]{1,0:T(8,128)(2,1)} %fusion.14.refs_0_), channel_id=1, source_target_pairs={{0,2},{1,3},{2,0},{3,1},{4,6},{5,7},{6,4},{7,5}} | collective-permute-start | bytes 2162696 | tf_op jit(solution)/shard_map/ppermute | solution.py:472
  349.8 24.5 %collective-permute-start.26 = (bf16[128,2816]{1,0:T(8,128)(2,1)}, bf16[128,2816]{1,0:T(8,128)(2,1)}, u32[]{:S(2)}, u32[]{:S(2)}) collective-permute-start(bf16[128,2816]{1,0:T(8,128)(2,1)} %fusion.14.refs_0_), channel_id=1, source_target_pairs={{0,1},{1,0},{2,3},{3,2},{4,5},{5,4},{6,7},{7,6}} | collective-permute-start | bytes 2162696 | tf_op jit(solution)/shard_map/ppermute | solution.py:472
  367.2 7.1 %collective-permute-start.27 = (bf16[128,2816]{1,0:T(8,128)(2,1)}, bf16[128,2816]{1,0:T(8,128)(2,1)}, u32[]{:S(2)}, u32[]{:S(2)}) collective-permute-start(bf16[128,2816]{1,0:T(8,128)(2,1)} %collective-permute-done.13.refs_2_), channel_id=1, source_target_pairs={{0,1},{1,0},{2,3},{3,2},{4,5},{5,4},{6,7},{7,6}} | collective-permute-start | bytes 2162696 | tf_op jit(solution)/shard_map/ppermute | solution.py:472
  367.2 7.1 %collective-permute-start.28 = (bf16[128,2816]{1,0:T(8,128)(2,1)}, bf16[128,2816]{1,0:T(8,128)(2,1)}, u32[]{:S(2)}, u32[]{:S(2)}) collective-permute-start(bf16[128,2816]{1,0:T(8,128)(2,1)} %collective-permute-done.14.refs_3_), channel_id=1, source_target_pairs={{0,1},{1,0},{2,3},{3,2},{4,5},{5,4},{6,7},{7,6}} | collective-permute-start | bytes 2162696 | tf_op jit(solution)/shard_map/ppermute | solution.py:472
  372.2 18.4 %collective-permute-start.24 = (bf16[352,1024]{1,0:T(8,128)(2,1)}, bf16[352,1024]{1,0:T(8,128)(2,1)}, u32[]{:S(2)}, u32[]{:S(2)}) collective-permute-start(bf16[352,1024]{1,0:T(8,128)(2,1)} %fusion.17.refs_0_), channel_id=1, source_target_pairs={{0,4},{1,5},{2,6},{3,7},{4,0},{5,1},{6,2},{7,3}} | collective-permute-start | bytes 2162696 | tf_op jit(solution)/shard_map/ppermute | solution.py:472
  372.8 18.1 %collective-permute-start.25 = (bf16[352,1024]{1,0:T(8,128)(2,1)}, bf16[352,1024]{1,0:T(8,128)(2,1)}, u32[]{:S(2)}, u32[]{:S(2)}) collective-permute-start(bf16[352,1024]{1,0:T(8,128)(2,1)} %fusion.17.refs_0_), channel_id=1, source_target_pairs={{0,2},{1,3},{2,0},{3,1},{4,6},{5,7},{6,4},{7,5}} | collective-permute-start | bytes 2162696 | tf_op jit(solution)/shard_map/ppermute | solution.py:472
  374.3 23.6 %collective-permute-start.23 = (bf16[352,1024]{1,0:T(8,128)(2,1)}, bf16[352,1024]{1,0:T(8,128)(2,1)}, u32[]{:S(2)}, u32[]{:S(2)}) collective-permute-start(bf16[352,1024]{1,0:T(8,128)(2,1)} %fusion.17.refs_0_), channel_id=1, source_target_pairs={{0,1},{1,0},{2,3},{3,2},{4,5},{5,4},{6,7},{7,6}} | collective-permute-start | bytes 2162696 | tf_op jit(solution)/shard_map/ppermute | solution.py:472
  390.9 8.5 %collective-permute-start.30 = (bf16[352,1024]{1,0:T(8,128)(2,1)}, bf16[352,1024]{1,0:T(8,128)(2,1)}, u32[]{:S(2)}, u32[]{:S(2)}) collective-permute-start(bf16[352,1024]{1,0:T(8,128)(2,1)} %collective-permute-done.25.refs_3_), channel_id=1, source_target_pairs={{0,1},{1,0},{2,3},{3,2},{4,5},{5,4},{6,7},{7,6}} | collective-permute-start | bytes 2162696 | tf_op jit(solution)/shard_map/ppermute | solution.py:472
  395.8 19.3 %collective-permute-start.21 = (bf16[352,1024]{1,0:T(8,128)(2,1)}, bf16[352,1024]{1,0:T(8,128)(2,1)}, u32[]{:S(2)}, u32[]{:S(2)}) collective-permute-start(bf16[352,1024]{1,0:T(8,128)(2,1)} %fusion.20.refs_0_), channel_id=1, source_target_pairs={{0,4},{1,5},{2,6},{3,7},{4,0},{5,1},{6,2},{7,3}} | collective-permute-start | bytes 2162696 | tf_op jit(solution)/shard_map/ppermute | solution.py:472
  397.2 18.1 %collective-permute-start.22 = (bf16[352,1024]{1,0:T(8,128)(2,1)}, bf16[352,1024]{1,0:T(8,128)(2,1)}, u32[]{:S(2)}, u32[]{:S(2)}) collective-permute-start(bf16[352,1024]{1,0:T(8,128)(2,1)} %fusion.20.refs_0_), channel_id=1, source_target_pairs={{0,2},{1,3},{2,0},{3,1},{4,6},{5,7},{6,4},{7,5}} | collective-permute-start | bytes 2162696 | tf_op jit(solution)/shard_map/ppermute | solution.py:472
  397.9 36.4 %collective-permute-start.20 = (bf16[352,1024]{1,0:T(8,128)(2,1)}, bf16[352,1024]{1,0:T(8,128)(2,1)}, u32[]{:S(2)}, u32[]{:S(2)}) collective-permute-start(bf16[352,1024]{1,0:T(8,128)(2,1)} %fusion.20.refs_0_), channel_id=1, source_target_pairs={{0,1},{1,0},{2,3},{3,2},{4,5},{5,4},{6,7},{7,6}} | collective-permute-start | bytes 2162696 | tf_op jit(solution)/shard_map/ppermute | solution.py:472
  397.9 36.4 %collective-permute-start.34 = (bf16[128,2816]{1,0:T(8,128)(2,1)}, bf16[128,2816]{1,0:T(8,128)(2,1)}, u32[]{:S(2)}, u32[]{:S(2)}) collective-permute-start(bf16[128,2816]{1,0:T(8,128)(2,1)} %collective-permute-done.4.refs_3_), channel_id=1, source_target_pairs={{0,4},{1,5},{2,6},{3,7},{4,0},{5,1},{6,2},{7,3}} | collective-permute-start | bytes 2162696 | tf_op jit(solution)/shard_map/ppermute | solution.py:472
  415.3 19.0 %collective-permute-start.31 = (bf16[352,1024]{1,0:T(8,128)(2,1)}, bf16[352,1024]{1,0:T(8,128)(2,1)}, u32[]{:S(2)}, u32[]{:S(2)}) collective-permute-start(bf16[352,1024]{1,0:T(8,128)(2,1)} %collective-permute-done.21.refs_2_), channel_id=1, source_target_pairs={{0,1},{1,0},{2,3},{3,2},{4,5},{5,4},{6,7},{7,6}} | collective-permute-start | bytes 2162696 | tf_op jit(solution)/shard_map/ppermute | solution.py:472
  415.3 19.0 %collective-permute-start.32 = (bf16[352,1024]{1,0:T(8,128)(2,1)}, bf16[352,1024]{1,0:T(8,128)(2,1)}, u32[]{:S(2)}, u32[]{:S(2)}) collective-permute-start(bf16[352,1024]{1,0:T(8,128)(2,1)} %collective-permute-done.22.refs_3_), channel_id=1, source_target_pairs={{0,1},{1,0},{2,3},{3,2},{4,5},{5,4},{6,7},{7,6}} | collective-permute-start | bytes 2162696 | tf_op jit(solution)/shard_map/ppermute | solution.py:472
  433.0 18.4 %collective-permute-start.19 = (bf16[128,2816]{1,0:T(8,128)(2,1)}, bf16[128,2816]{1,0:T(8,128)(2,1)}, u32[]{:S(2)}, u32[]{:S(2)}) collective-permute-start(bf16[128,2816]{1,0:T(8,128)(2,1)} %collective-permute-done.6.refs_2_), channel_id=1, source_target_pairs={{0,2},{1,3},{2,0},{3,1},{4,6},{5,7},{6,4},{7,5}} | collective-permute-start | bytes 2162696 | tf_op jit(solution)/shard_map/ppermute | solution.py:472
  434.3 21.4 %collective-permute-start.35 = (bf16[128,2816]{1,0:T(8,128)(2,1)}, bf16[128,2816]{1,0:T(8,128)(2,1)}, u32[]{:S(2)}, u32[]{:S(2)}) collective-permute-start(bf16[128,2816]{1,0:T(8,128)(2,1)} %collective-permute-done.34.refs_1_), channel_id=1, source_target_pairs={{0,1},{1,0},{2,3},{3,2},{4,5},{5,4},{6,7},{7,6}} | collective-permute-start | bytes 2162696 | tf_op jit(solution)/shard_map/ppermute | solution.py:472
  451.3 18.9 %collective-permute-start.12 = (bf16[128,2816]{1,0:T(8,128)(2,1)}, bf16[128,2816]{1,0:T(8,128)(2,1)}, u32[]{:S(2)}, u32[]{:S(2)}) collective-permute-start(bf16[128,2816]{1,0:T(8,128)(2,1)} %collective-permute-done.refs_2_), channel_id=1, source_target_pairs={{0,2},{1,3},{2,0},{3,1},{4,6},{5,7},{6,4},{7,5}} | collective-permute-start | bytes 2162696 | tf_op jit(solution)/shard_map/ppermute | solution.py:472
  452.7 18.6 %collective-permute-start.18 = (bf16[128,2816]{1,0:T(8,128)(2,1)}, bf16[128,2816]{1,0:T(8,128)(2,1)}, u32[]{:S(2)}, u32[]{:S(2)}) collective-permute-start(bf16[128,2816]{1,0:T(8,128)(2,1)} %collective-permute-done.14.refs_3_), channel_id=1, source_target_pairs={{0,4},{1,5},{2,6},{3,7},{4,0},{5,1},{6,2},{7,3}} | collective-permute-start | bytes 2162696 | tf_op jit(solution)/shard_map/ppermute | solution.py:472
  471.8 18.4 %collective-permute-start.36 = (bf16[352,1024]{1,0:T(8,128)(2,1)}, bf16[352,1024]{1,0:T(8,128)(2,1)}, u32[]{:S(2)}, u32[]{:S(2)}) collective-permute-start(bf16[352,1024]{1,0:T(8,128)(2,1)} %collective-permute-done.24.refs_2_), channel_id=1, source_target_pairs={{0,2},{1,3},{2,0},{3,1},{4,6},{5,7},{6,4},{7,5}} | collective-permute-start | bytes 2162696 | tf_op jit(solution)/shard_map/ppermute | solution.py:472
  472.5 18.1 %collective-permute-start.37 = (bf16[352,1024]{1,0:T(8,128)(2,1)}, bf16[352,1024]{1,0:T(8,128)(2,1)}, u32[]{:S(2)}, u32[]{:S(2)}) collective-permute-start(bf16[352,1024]{1,0:T(8,128)(2,1)} %collective-permute-done.22.refs_3_), channel_id=1, source_target_pairs={{0,4},{1,5},{2,6},{3,7},{4,0},{5,1},{6,2},{7,3}} | collective-permute-start | bytes 2162696 | tf_op jit(solution)/shard_map/ppermute | solution.py:472
  (17 other events, 163.6 us)
